TPU v7x, 32 devices: a whole 2x2x4 slice. The times are simulated.
32 devices in a mesh: gx: 4 (over y, x), gy: 2 (over core), gz: 4 (over z).
Axes of the slice: x: 2, y: 2, z: 4, core: 2. Of those that a mesh axis runs over, the one named last changes fastest.
Arguments:
- labels: int32 [128, 128, 512], P('gx', 'gy', 'gz'), may hold values from 0 to 7
- conductivity: float32 [7, 8], replicated, may hold values from -0.08 to 2, as said below
- right_side: float32 [128, 128, 512], P('gx', 'gy', 'gz'), may hold values from -18 to 18
Outputs:
- solution: float32 [128, 128, 512], P('gx', 'gy', 'gz')
Inputs may be any that keep to these rules, and one draw needn't show every extreme that they name: `conductivity`: rows 0 to 2 are positive, rows 3 to 5 have magnitude at most 0.08, row 6 is at least 0.5.
All inputs are finite; a program needn't handle non-finite values.
Results may differ from a plain program's by a relative error of at most 0.0001.
Values sent between devices are 32-bit elements; how exact they have to be, the bound alone decides.
A program may use at most 128 MiB of HBM per device.

v0:
```python
import functools
import itertools
import math
import jax
import jax.numpy as jnp
from jax import lax
from jax.experimental import pallas as pl
from jax.experimental.pallas import tpu as pltpu
from jax.sharding import PartitionSpec as P

ITERS = 3
AXES = ("gx", "gy", "gz")
ROUNDS = ITERS + 1
MOMENTS = 2 * ITERS
LANES = 128
PAD = 8
CH = 16


def kernel(
    sizes, lab_hbm, cond, rhs_hbm, out, lab, rhs, V0, V1, V2, V3, S, DI, PS, PR, ES, ER, HB, HS, PG, CP, MA, RS, RR,
    send_sem, recv_sem, ar_send, ar_recv, in_sem,
):
    V = (V0, V1, V2, V3)
    X, Y, Z = rhs.shape
    lab_copy = pltpu.make_async_copy(lab_hbm, lab, in_sem.at[0])
    lab_copy.start()
    rhs_copy = pltpu.make_async_copy(rhs_hbm, rhs, in_sem.at[1])
    rhs_copy.start()
    YE = Y + 2 * PAD
    TOP = PAD + Y
    me = [lax.axis_index(a) for a in AXES]
    f32 = jnp.float32

    directions = []
    for dx in (-1, 0, 1):
        for dy in (-1, 0, 1):
            for dz in (-1, 0, 1):
                d = (dx, dy, dz)
                live = sum(1 for t in d if t)
                if live in (1, 2) and all(n > 1 for t, n in zip(d, sizes) if t):
                    directions.append(d)

    def present(d):
        ok = None
        for t, m, n in zip(d, me, sizes):
            if t == 0:
                continue
            here = (m < n - 1) if t > 0 else (m > 0)
            ok = here if ok is None else jnp.logical_and(ok, here)
        return ok

    def places(d, r):
        dx, dy, dz = d
        rows_from = pl.ds(PAD, Y) if dy == 0 else (pl.ds(TOP - 8, 8) if dy > 0 else pl.ds(PAD, 8))
        rows_to = pl.ds(PAD, Y) if dy == 0 else (pl.ds(0, 8) if dy > 0 else pl.ds(TOP, 8))
        if dz == 0:
            if dx == 0:
                return V[r].at[pl.ds(1, X), rows_from], V[r].at[pl.ds(1, X), rows_to]
            fx, tx = (X, 0) if dx > 0 else (1, X + 1)
            return V[r].at[fx, rows_from], V[r].at[tx, rows_to]
        side = 0 if dz > 0 else 1
        if dx == 0:
            return PS.at[r, rows_from], PR.at[r, side, rows_to]
        slot = (0 if dx > 0 else 2) + side
        return ES.at[r], ER.at[r, slot]

    def copy(d, r):
        src, dst = places(d, r)
        m = directions.index(d)
        return pltpu.make_async_remote_copy(
            src_ref=src,
            dst_ref=dst,
            send_sem=send_sem.at[r, m],
            recv_sem=recv_sem.at[r, m],
            device_id=tuple(a + t for a, t in zip(me, d)),
            device_id_type=pl.DeviceIdType.MESH,
        )

    groups = [(0, 1, 2)] if math.prod(sizes) <= 32 else [(0, 1), (2,)]

    def offsets(group):
        ranges = [range(n) if i in group else (0,) for i, n in enumerate(sizes)]
        return [t for t in itertools.product(*ranges) if any(t)]

    def partner(t):
        return tuple(lax.rem(m + k, n) for m, k, n in zip(me, t, sizes))

    barrier = pltpu.get_barrier_semaphore()
    greeted = 0
    for group in groups:
        for t in offsets(group):
            pl.semaphore_signal(
                barrier, inc=1, device_id=partner(t), device_id_type=pl.DeviceIdType.MESH
            )
            greeted += 1
    if len(groups) > 1:
        for d in directions:
            pl.when(present(d))(
                lambda d=d: pl.semaphore_signal(
                    barrier,
                    inc=1,
                    device_id=tuple(a + t for a, t in zip(me, d)),
                    device_id_type=pl.DeviceIdType.MESH,
                )
            )
            greeted = greeted + jnp.where(present(d), 1, 0)

    for d in [
        (dx, dy, dz)
        for dx in (-1, 0, 1)
        for dy in (-1, 0, 1)
        for dz in (-1, 0, 1)
        if sum(1 for t in (dx, dy, dz) if t) in (1, 2)
    ]:
        def clear(d=d):
            for r in range(ROUNDS):
                _, dst = places(d, r)
                dst[...] = jnp.zeros(dst.shape, f32)

        if d in directions:
            back = tuple(-t for t in d)
            pl.when(jnp.logical_not(present(back)))(clear)
        else:
            clear()

    def start(r):
        lane8 = lax.broadcasted_iota(jnp.int32, (8, LANES), 1)
        tile = jnp.zeros((8, LANES), f32)
        for col, at in enumerate((0, LANES - 1, 2 * (X - 1), 2 * (X - 1) - 1)):
            for k in range(Y // 8):
                to = col * (Y // 8) + k
                part = PS[r, pl.ds(PAD + 8 * k, 8), :]
                tile = jnp.where(lane8 == to, pltpu.roll(part, (to - at) % LANES, 1), tile)
        ES[r] = tile
        for d in directions:
            pl.when(present(d))(lambda d=d: copy(d, r).start())

    def wait(r):
        for d in directions:
            back = tuple(-t for t in d)
            pl.when(present(back))(lambda d=d: copy(d, r).wait_recv())

    lane_e = lax.broadcasted_iota(jnp.int32, (YE, LANES), 1)
    lane_c = lax.broadcasted_iota(jnp.int32, (CH, LANES), 1)
    lane_8 = lax.broadcasted_iota(jnp.int32, (8, LANES), 1)
    even = lane_e % 2 == 0
    lane_y = lax.broadcasted_iota(jnp.int32, (Y, LANES), 1)

    def build_halo(r):
        low = pltpu.roll(PR[r, 0], 1, 1)
        high = pltpu.roll(PR[r, 1], LANES - 1, 1)
        valid = jnp.logical_or(lane_e <= 2 * (X - 1), lane_e == LANES - 1)
        HB[...] = jnp.where(valid, jnp.where(even, low, high), 0.0)
        targets = (((LANES - 2), 3), ((LANES - 3), 2), (2 * X, 1), (2 * X - 1, 0))
        tiles = [ER[r, slot] for slot in range(4)]
        for k in range(Y // 8):
            rows = pl.ds(PAD + 8 * k, 8)
            part = HB[rows, :]
            for slot, (target, col) in enumerate(targets):
                at = col * (Y // 8) + k
                part = jnp.where(
                    lane_8 == target, pltpu.roll(tiles[slot], (target - at) % LANES, 1), part
                )
            HB[rows, :] = part

    def zm(a):
        return jnp.where(lane_c == 0, 0.0, pltpu.roll(a, 1, 1))

    def zp(a):
        return jnp.where(lane_c == LANES - 1, 0.0, pltpu.roll(a, LANES - 1, 1))

    def unpack(x, a):
        part = pltpu.roll(CP[pl.ds(a, CH), :], lax.rem(LANES - 2 * x, LANES), 1)
        return jnp.where(jnp.logical_or(lane_c == 0, lane_c == LANES - 1), part, 0.0)

    def pack(r):
        @pl.loop(0, Y // 8, unroll=4)
        def _(k):
            rows = pl.ds(pl.multiple_of(PAD + 8 * k, 8), 8)
            parts = [V[r][x + 1, rows, :] for x in range(X)]
            width = 1
            while len(parts) > 1:
                joined = []
                for i in range(0, len(parts), 2):
                    low = parts[i]
                    if i + 1 < len(parts):
                        keep = jnp.logical_or(lane_8 <= 2 * width - 2, lane_8 == LANES - 1)
                        low = jnp.where(keep, low, pltpu.roll(parts[i + 1], 2 * width, 1))
                    joined.append(low)
                parts = joined
                width *= 2
            PS[r, rows, :] = parts[0]

    scale = (0.5, 0.5, 0.5, 0.25, 0.25, 0.25)
    count = cond.shape[1]
    table = [[cond[c, k] * scale[c] for k in range(count)] for c in range(6)]
    self_row = [cond[6, k] for k in range(count)]

    def lookup(values, components):
        outs = [jnp.zeros(values.shape, f32) for _ in components]
        for k in range(count):
            hit = values == f32(k + 1)
            outs = [
                jnp.where(hit, (self_row if c == 6 else table[c])[k], o)
                for c, o in zip(components, outs)
            ]
        return outs

    PS[...] = jnp.zeros(PS.shape, f32)
    lab_copy.wait()
    MA[...] = jnp.zeros(MA.shape, f32)
    chunks = [PAD + i for i in range(0, Y, CH)]

    @pl.loop(0, X)
    def _(x):
        for a in chunks:
            value = (lab[x, pl.ds(a - PAD, CH), :] + 1).astype(f32)
            V[0][x + 1, pl.ds(a, CH), :] = value

    pack(0)
    pl.semaphore_wait(barrier, greeted)
    start(0)
    wait(0)

    @pl.loop(0, X + 2, unroll=2)
    def _(x):
        for a in range(0, YE, CH):
            for c, s in enumerate(lookup(V[0][x, pl.ds(a, CH), :], range(6))):
                S[c, x, pl.ds(a, CH), :] = s

    build_halo(0)
    for i, s in enumerate(lookup(HB[...], (2, 4, 5))):
        HS[i] = s
    for i, s in enumerate(lookup(PS[0], (2, 4, 5))):
        PG[i] = s
    CP[...] = HS[0]
    rhs_copy.wait()

    def gather8(value):
        total = value[0:8]
        for i in range(8, CH, 8):
            total = total + value[i : i + 8]
        return total

    @pl.loop(0, X, unroll=4)
    def _(x):
        total = jnp.zeros((8, LANES), f32)
        for a in chunks:
            rows = pl.ds(a, CH)
            own = pl.ds(a - PAD, CH)
            (s6,) = lookup(V[0][x + 1, rows, :], (6,))
            s0, s1, s2 = (S[c, x + 1, rows, :] for c in range(3))
            diag = s6 + 2.0 * (s0 + s1 + s2)
            diag = diag + S[0, x, rows, :] + S[0, x + 2, rows, :]
            diag = diag + S[1, x + 1, pl.ds(a - 1, CH), :] + S[1, x + 1, pl.ds(a + 1, CH), :]
            diag = diag + zm(s2) + zp(s2) + unpack(x, a)
            inverse = 1.0 / diag
            DI[x, own, :] = inverse
            r0 = rhs[x, own, :]
            w = r0 * inverse
            V[1][x + 1, rows, :] = w
            total = total + gather8(r0 * w)
        MA[0] = MA[0] + total

    for step in range(ITERS):
        r = step + 1
        pack(r)
        start(r)
        wait(r)
        build_halo(r)
        sign = jnp.where(even, f32(-1.0), f32(1.0))

        def along_x(a):
            return pltpu.roll(a, LANES - 2, 1) - pltpu.roll(a, 2, 1)

        def along_y(a):
            return pltpu.roll(a, YE - 1, 0) - pltpu.roll(a, 1, 0)

        h = HB[...]
        CP[...] = (PG[0] + HS[0]) * h + sign * (
            PG[1] * along_x(h) + along_x(HS[1] * h) + PG[2] * along_y(h) + along_y(HS[2] * h)
        )
        last = step + 1 == ITERS

        @pl.loop(0, X, unroll=4)
        def _(x):
            odd = jnp.zeros((8, LANES), f32)
            evn = jnp.zeros((8, LANES), f32)
            for a in chunks:
                rows, up, down = pl.ds(a, CH), pl.ds(a + 1, CH), pl.ds(a - 1, CH)
                own = pl.ds(a - PAD, CH)
                v = V[r][x + 1, rows, :]
                vu, vd = V[r][x + 1, up, :], V[r][x + 1, down, :]
                p, pu, pd = V[r][x + 2, rows, :], V[r][x + 2, up, :], V[r][x + 2, down, :]
                m, mu, md = V[r][x, rows, :], V[r][x, up, :], V[r][x, down, :]
                dx = p - m
                dy = vu - vd
                q = S[0, x + 1, rows, :] * (m + p) + S[0, x, rows, :] * m + S[0, x + 2, rows, :] * p
                q = q + S[1, x + 1, rows, :] * (vu + vd)
                q = q + S[1, x + 1, up, :] * vu + S[1, x + 1, down, :] * vd
                q = q + S[3, x + 1, rows, :] * ((pu - pd) - (mu - md))
                q = q + (S[3, x + 2, up, :] * pu - S[3, x + 2, down, :] * pd)
                q = q - (S[3, x, up, :] * mu - S[3, x, down, :] * md)
                s2 = S[2, x + 1, rows, :]
                q = q + s2 * (zp(v) + zm(v))
                q = q + S[4, x + 1, rows, :] * (zp(dx) - zm(dx))
                q = q + S[5, x + 1, rows, :] * (zp(dy) - zm(dy))
                u = s2 * v
                g = S[4, x + 2, rows, :] * p - S[4, x, rows, :] * m
                g = g + S[5, x + 1, up, :] * vu - S[5, x + 1, down, :] * vd
                q = q + zp(u + g) + zm(u - g)
                q = q + unpack(x, a)
                odd = odd + gather8(v * q)
                if not last:
                    w = q * DI[x, own, :]
                    evn = evn + gather8(w * q)
                    V[r + 1][x + 1, rows, :] = w
            MA[2 * step + 1] = MA[2 * step + 1] + odd
            if not last:
                MA[2 * step + 2] = MA[2 * step + 2] + evn

    row = lax.broadcasted_iota(jnp.int32, (8, LANES), 0)
    tile = jnp.zeros((8, LANES), f32)
    for k in range(MOMENTS):
        tile = jnp.where(row == k, jnp.sum(MA[k], axis=0, keepdims=True), tile)
    for order, group in enumerate(groups):
        slot = 0
        members = 1
        for i in group:
            slot = slot * sizes[i] + me[i]
            members *= sizes[i]
        RS[order] = tile
        copies = []
        for index, t in enumerate(offsets(group)):
            c = pltpu.make_async_remote_copy(
                src_ref=RS.at[order],
                dst_ref=RR.at[order, slot],
                send_sem=ar_send.at[order, index],
                recv_sem=ar_recv.at[order, index],
                device_id=partner(t),
                device_id_type=pl.DeviceIdType.MESH,
            )
            c.start()
            copies.append(c)
        RR[order, slot] = tile
        for c in copies:
            c.wait()
        parts = [RR[order, t] for t in range(members)]
        while len(parts) > 1:
            parts = [sum(parts[i + 1 : i + 2], parts[i]) for i in range(0, len(parts), 2)]
        tile = parts[0]

    n0, n1, n2, n3, n4, n5 = (
        jnp.sum(tile[k : k + 1], axis=1, keepdims=True) for k in range(MOMENTS)
    )

    def inverse_of(d):
        return jnp.where(d > 0.0, 1.0 / d, 0.0)

    g00, g01, g02, g12, g22 = n0 - n1, n1 - n2, n2 - n3, n3 - n4, n4 - n5
    i0 = 1.0 / g00
    l1, l2 = g01 * i0, g02 * i0
    i1 = inverse_of(g02 - l1 * g01)
    e = g12 - l2 * g01
    l21 = e * i1
    i2 = inverse_of(g22 - l2 * g02 - l21 * e)
    y1 = n1 - l1 * n0
    y2 = n2 - l2 * n0 - l21 * y1
    c2 = y2 * i2
    c1 = y1 * i1 - l21 * c2
    c0 = n0 * i0 - l1 * c1 - l2 * c2

    @pl.loop(0, X)
    def _(x):
        for a in chunks:
            rows = pl.ds(a, CH)
            out[x, pl.ds(a - PAD, CH), :] = (
                c0 * V[1][x + 1, rows, :] + c1 * V[2][x + 1, rows, :] + c2 * V[3][x + 1, rows, :]
            )

    for r in range(ROUNDS):
        for d in directions:
            pl.when(present(d))(lambda d=d, r=r: copy(d, r).wait_send())


def solution(mesh):
    sizes = tuple(mesh.shape[a] for a in AXES)

    def local(labels, conductivity, right_side):
        X, Y, Z = right_side.shape
        YE = Y + 2 * PAD
        f32 = jnp.float32
        vmem = pltpu.VMEM
        return pl.pallas_call(
            functools.partial(kernel, sizes),
            out_shape=jax.ShapeDtypeStruct((X, Y, Z), f32),
            in_specs=[
                pl.BlockSpec(memory_space=pl.ANY),
                pl.BlockSpec(memory_space=pltpu.SMEM),
                pl.BlockSpec(memory_space=pl.ANY),
            ],
            out_specs=pl.BlockSpec(memory_space=pltpu.VMEM),
            scratch_shapes=[
                vmem((X, Y, Z), jnp.int32),
                vmem((X, Y, Z), f32),
                vmem((X + 2, YE, Z), f32),
                vmem((X + 2, YE, Z), f32),
                vmem((X + 2, YE, Z), f32),
                vmem((X + 2, YE, Z), f32),
                vmem((6, X + 2, YE, Z), f32),
                vmem((X, Y, Z), f32),
                vmem((ROUNDS, YE, Z), f32),
                vmem((ROUNDS, 2, YE, Z), f32),
                vmem((ROUNDS, 8, Z), f32),
                vmem((ROUNDS, 4, 8, Z), f32),
                vmem((YE, Z), f32),
                vmem((3, YE, Z), f32),
                vmem((3, YE, Z), f32),
                vmem((YE, Z), f32),
                vmem((MOMENTS, 8, Z), f32),
                vmem((2, 8, Z), f32),
                vmem((2, 32, 8, Z), f32),
                pltpu.SemaphoreType.DMA((ROUNDS, 18)),
                pltpu.SemaphoreType.DMA((ROUNDS, 18)),
                pltpu.SemaphoreType.DMA((2, 32)),
                pltpu.SemaphoreType.DMA((2, 32)),
                pltpu.SemaphoreType.DMA((2,)),
            ],
            compiler_params=pltpu.CompilerParams(
                collective_id=0, has_side_effects=True, vmem_limit_bytes=60 * 1024 * 1024
            ),
        )(labels, conductivity, right_side)

    return jax.shard_map(
        local,
        mesh=mesh,
        in_specs=(P("gx", "gy", "gz"), P(), P("gx", "gy", "gz")),
        out_specs=P("gx", "gy", "gz"),
        check_vma=False,
    )
```

profile of v0, /device:TPU:0, one launch (start us, length us, event | category | flops | bytes accessed | tf_op | source)
XLA Modules:
  0.0 53.2 jit_solution(4163912555919488606)
XLA Ops:
  0.0 50.8 %shard_map.37 = f32[32,64,128]{2,1,0:T(8,128)} custom-call(s32[32,64,128]{2,1,0:T(8,128)} %lab_hbm.1, f32[7,8]{1,0:T(8,128)} %cond.1, f32[32,64,128]{2,1,0:T(8,128)} %rhs_hbm.1), custom_call_target="tpu_custom_call" | custom-call | tf_op jit(solution)/shard_map/pallas_call | solution.py:395
  50.8 2.3 %copy.5 = f32[32,64,128]{2,1,0:T(8,128)} copy(f32[32,64,128]{2,1,0:T(8,128)} %shard_map.37) | data formatting | bytes 2097152
where the time goes:
time: 53.4 us; the launch traced here: 53.2 us
  Pallas kernels  50.8 us (95%)
  local copies, waits for them, and re-layouts  2.31 us (4%)
    pallas_call x1, Pallas kernels, local(): pl.pallas_call(functools.partial(kernel, sizes), out_shape=jax.ShapeDtype...  50.8 us
    unnamed x1, local copies, waits for them, and re-layouts  2.31 us

commit v1 on v0

v1 whole, which is shorter than its diff:
```python
import functools
import itertools
import math
import jax
import jax.numpy as jnp
from jax import lax
from jax.experimental import pallas as pl
from jax.experimental.pallas import tpu as pltpu
from jax.sharding import PartitionSpec as P

ITERS = 3
AXES = ("gx", "gy", "gz")
ROUNDS = ITERS + 1
MOMENTS = 2 * ITERS
LANES = 128
PAD = 8
T8 = 8


def group_size(n, most):
    return max(u for u in range(1, most + 1) if n % u == 0)


def kernel(
    sizes, lab_hbm, cond, rhs_hbm, out, lab, rhs, V0, V1, V2, V3, S, F, DI, PS, PR, ES, ER, HB, HS, PG, CP, MA, RS,
    RR, send_sem, recv_sem, ar_send, ar_recv, in_sem,
):
    V = (V0, V1, V2, V3)
    X, Y, Z = rhs.shape
    lab_copy = pltpu.make_async_copy(lab_hbm, lab, in_sem.at[0])
    lab_copy.start()
    rhs_copy = pltpu.make_async_copy(rhs_hbm, rhs, in_sem.at[1])
    rhs_copy.start()
    YE = Y + 2 * PAD
    TOP = PAD + Y
    KT = Y // T8
    me = [lax.axis_index(a) for a in AXES]
    f32 = jnp.float32
    scope = jax.named_scope

    directions = []
    for dx in (-1, 0, 1):
        for dy in (-1, 0, 1):
            for dz in (-1, 0, 1):
                d = (dx, dy, dz)
                live = sum(1 for t in d if t)
                if live in (1, 2) and all(n > 1 for t, n in zip(d, sizes) if t):
                    directions.append(d)

    def needed(d, r):
        if r < ROUNDS - 1:
            return True
        if d[2]:
            return d[2] < 0
        return d[0] <= 0 and d[1] <= 0

    def present(d):
        ok = None
        for t, m, n in zip(d, me, sizes):
            if t == 0:
                continue
            here = (m < n - 1) if t > 0 else (m > 0)
            ok = here if ok is None else jnp.logical_and(ok, here)
        return ok

    def places(d, r):
        dx, dy, dz = d
        rows_from = pl.ds(PAD, Y) if dy == 0 else (pl.ds(TOP - 8, 8) if dy > 0 else pl.ds(PAD, 8))
        rows_to = pl.ds(PAD, Y) if dy == 0 else (pl.ds(0, 8) if dy > 0 else pl.ds(TOP, 8))
        if dz == 0:
            if dx == 0:
                return V[r].at[pl.ds(1, X), rows_from], V[r].at[pl.ds(1, X), rows_to]
            fx, tx = (X, 0) if dx > 0 else (1, X + 1)
            return V[r].at[fx, rows_from], V[r].at[tx, rows_to]
        side = 0 if dz > 0 else 1
        if dx == 0:
            return PS.at[r, rows_from], PR.at[r, side, rows_to]
        slot = (0 if dx > 0 else 2) + side
        return ES.at[r], ER.at[r, slot]

    def copy(d, r):
        src, dst = places(d, r)
        m = directions.index(d)
        return pltpu.make_async_remote_copy(
            src_ref=src,
            dst_ref=dst,
            send_sem=send_sem.at[r, m],
            recv_sem=recv_sem.at[r, m],
            device_id=tuple(a + t for a, t in zip(me, d)),
            device_id_type=pl.DeviceIdType.MESH,
        )

    groups = [(0, 1, 2)] if math.prod(sizes) <= 32 else [(0, 1), (2,)]
    near = len(groups) == 1 and max(sizes) <= ROUNDS and sum(n - 1 for n in sizes) <= 2 * ROUNDS - 1

    def offsets(group):
        ranges = [range(n) if i in group else (0,) for i, n in enumerate(sizes)]
        return [t for t in itertools.product(*ranges) if any(t)]

    def partner(t):
        return tuple(lax.rem(m + k, n) for m, k, n in zip(me, t, sizes))

    barrier = pltpu.get_barrier_semaphore()
    greeted = 0
    if not near:
        for group in groups:
            for t in offsets(group):
                pl.semaphore_signal(
                    barrier, inc=1, device_id=partner(t), device_id_type=pl.DeviceIdType.MESH
                )
                greeted += 1
    if near or len(groups) > 1:
        for d in directions:
            pl.when(present(d))(
                lambda d=d: pl.semaphore_signal(
                    barrier,
                    inc=1,
                    device_id=tuple(a + t for a, t in zip(me, d)),
                    device_id_type=pl.DeviceIdType.MESH,
                )
            )
            greeted = greeted + jnp.where(present(d), 1, 0)

    for d in [
        (dx, dy, dz)
        for dx in (-1, 0, 1)
        for dy in (-1, 0, 1)
        for dz in (-1, 0, 1)
        if sum(1 for t in (dx, dy, dz) if t) in (1, 2)
    ]:
        def clear(d=d):
            for r in range(ROUNDS):
                if needed(d, r):
                    _, dst = places(d, r)
                    dst[...] = jnp.zeros(dst.shape, f32)

        if d in directions:
            back = tuple(-t for t in d)
            pl.when(jnp.logical_not(present(back)))(clear)
        else:
            clear()

    for r in range(ROUNDS):
        for a in (0, TOP):
            PS[r, pl.ds(a, PAD), :] = jnp.zeros((PAD, LANES), f32)
    MA[...] = jnp.zeros(MA.shape, f32)

    lane_e = lax.broadcasted_iota(jnp.int32, (YE, LANES), 1)
    lane_8 = lax.broadcasted_iota(jnp.int32, (T8, LANES), 1)
    row_8 = lax.broadcasted_iota(jnp.int32, (T8, LANES), 0)
    even = lane_e % 2 == 0
    ends = jnp.logical_or(lane_8 == 0, lane_8 == LANES - 1)
    inner = lane_8 < LANES - 1
    tiles = [PAD + T8 * k for k in range(KT)]

    scale = (0.5, 0.5, 0.5, 0.25, 0.25, 0.25, 1.0)
    count = cond.shape[1]
    tables = []
    for c in range(7):
        table = jnp.zeros((T8, LANES), f32)
        for k in range(count):
            table = jnp.where(row_8 == k, cond[c, k] * scale[c], table)
        tables.append(table)

    def look(c, index):
        return jnp.take_along_axis(tables[c], index, axis=0, mode="promise_in_bounds")

    def look_known(values, components):
        index = jnp.maximum(values.astype(jnp.int32) - 1, 0)
        hit = values > 0.0
        return [jnp.where(hit, look(c, index), 0.0) for c in components]

    def send(d, r):
        if d in directions and needed(d, r):
            pl.when(present(d))(lambda: copy(d, r).start())

    def start_x(r, plane):
        tile = jnp.zeros((T8, LANES), f32)
        for col, (x, at) in enumerate(((0, 0), (0, LANES - 1), (X - 1, 0), (X - 1, LANES - 1))):
            for k in range(KT):
                to = col * KT + k
                part = plane(x, k)
                tile = jnp.where(lane_8 == to, pltpu.roll(part, (to - at) % LANES, 1), tile)
        ES[r] = tile
        for d in directions:
            if d[0]:
                send(d, r)

    def start_rest(r):
        for d in directions:
            if not d[0]:
                send(d, r)

    def wait(r):
        for d in directions:
            if needed(d, r):
                back = tuple(-t for t in d)
                pl.when(present(back))(lambda d=d: copy(d, r).wait_recv())

    def build_halo(r):
        low = pltpu.roll(PR[r, 0], 1, 1)
        high = pltpu.roll(PR[r, 1], LANES - 1, 1)
        valid = jnp.logical_or(lane_e <= 2 * (X - 1), lane_e == LANES - 1)
        last = r == ROUNDS - 1
        HB[...] = jnp.where(valid, jnp.where(even, 0.0 if last else low, high), 0.0)
        targets = (((LANES - 2), 3), ((LANES - 3), 2), (2 * X, 1), (2 * X - 1, 0))
        slots = (1, 3) if last else (0, 1, 2, 3)
        got = {slot: ER[r, slot] for slot in slots}
        for k in range(KT):
            rows = pl.ds(PAD + T8 * k, T8)
            part = HB[rows, :]
            for slot in slots:
                target, col = targets[slot]
                at = col * KT + k
                part = jnp.where(
                    lane_8 == target, pltpu.roll(got[slot], (target - at) % LANES, 1), part
                )
            HB[rows, :] = part

    def zm(a):
        return pltpu.roll(a, 1, 1)

    def zp(a):
        return pltpu.roll(a, LANES - 1, 1)

    def unpack(part, x):
        return jnp.where(ends, pltpu.roll(part, lax.rem(LANES - 2 * x, LANES), 1), 0.0)

    def pack(r, plane):
        for k in range(KT):
            tile = plane(0, k)
            for x in range(1, X):
                here = jnp.logical_and(lane_8 >= 2 * x - 1, inner)
                tile = jnp.where(here, pltpu.roll(plane(x, k), 2 * x, 1), tile)
            PS[r, pl.ds(PAD + T8 * k, T8), :] = tile

    def label_tile(x, k):
        return (lab[x, pl.ds(T8 * k, T8), :] + 1).astype(f32)

    def field_tile(r):
        return lambda x, k: V[r][x + 1, pl.ds(PAD + T8 * k, T8), :]

    with scope("labwait"):
        lab_copy.wait()

    with scope("conv"):
        for x in (0, X - 1):
            for k in range(KT):
                V[0][x + 1, pl.ds(PAD + T8 * k, T8), :] = label_tile(x, k)

        for x in range(1, X - 1):
            for k in (0, KT - 1):
                V[0][x + 1, pl.ds(PAD + T8 * k, T8), :] = label_tile(x, k)

    with scope("pack0"):
        pack(0, label_tile)
    with scope("barrier"):
        pl.semaphore_wait(barrier, greeted)
    with scope("start0"):
        start_x(0, label_tile)
        start_rest(0)

    with scope("sigma_own"):
        @pl.loop(0, X, unroll=4)
        def _(x):
            for a in tiles:
                index = lab[x, pl.ds(a - PAD, T8), :]
                for c in range(6):
                    S[c, x + 1, pl.ds(a, T8), :] = look(c, index)

    with scope("wait0"):
        wait(0)

    with scope("sigma_halo"):
        for x in (0, X + 1):
            for a in range(0, YE, T8):
                rows = pl.ds(a, T8)
                for c, s in enumerate(look_known(V[0][x, rows, :], range(6))):
                    S[c, x, rows, :] = s

        @pl.loop(1, X + 1, unroll=4)
        def _(x):
            for a in (0, TOP):
                rows = pl.ds(a, T8)
                for c, s in enumerate(look_known(V[0][x, rows, :], range(6))):
                    S[c, x, rows, :] = s

        build_halo(0)
        for a in range(0, YE, T8):
            rows = pl.ds(a, T8)
            for i, s in enumerate(look_known(HB[rows, :], (2, 4, 5))):
                HS[i, rows, :] = s
            for i, s in enumerate(look_known(PS[0, rows, :], (2, 4, 5))):
                PG[i, rows, :] = s
        CP[...] = PG[0] + HS[0]
        rhs_copy.wait()

    def coefficients(p):
        for a in [0] + tiles:
            rows, up = pl.ds(a, T8), pl.ds(a + 1, T8)
            s1, s1u = S[1, p, rows, :], S[1, p, up, :]
            s3, s3u = S[3, p, rows, :], S[3, p, up, :]
            t3, t3u = S[3, p + 1, rows, :], S[3, p + 1, up, :]
            s5, s5u = S[5, p, rows, :], S[5, p, up, :]
            F[1, p, rows, :] = s1 + s1u
            F[3, p, rows, :] = s3 + t3u
            F[4, p, rows, :] = t3 + s3u
            F[7, p, rows, :] = jnp.where(inner, s5 + zp(s5u), 0.0)
            F[8, p, rows, :] = jnp.where(inner, s5u + zp(s5), 0.0)
            if a:
                s2 = S[2, p, rows, :]
                s4, t4 = S[4, p, rows, :], S[4, p + 1, rows, :]
                F[0, p, rows, :] = S[0, p, rows, :] + S[0, p + 1, rows, :]
                F[2, p, rows, :] = jnp.where(inner, s2 + zp(s2), 0.0)
                F[5, p, rows, :] = jnp.where(inner, s4 + zp(t4), 0.0)
                F[6, p, rows, :] = jnp.where(inner, t4 + zp(s4), 0.0)

    def diagonal(x, total):
        p = x + 1
        for a in tiles:
            rows, down = pl.ds(a, T8), pl.ds(a - 1, T8)
            own = pl.ds(a - PAD, T8)
            f2 = F[2, p, rows, :]
            diag = look(6, lab[x, own, :]) + F[0, p, rows, :] + F[0, p - 1, rows, :]
            diag = diag + F[1, p, rows, :] + F[1, p, down, :]
            diag = diag + (f2 + zm(f2)) + unpack(CP[rows, :], x)
            inverse = 1.0 / diag
            DI[x, own, :] = inverse
            r0 = rhs[x, own, :]
            w = r0 * inverse
            V[1][p, rows, :] = w
            total = total + r0 * w
        return total

    def zero():
        return jnp.zeros((T8, LANES), f32)

    with scope("coef_x"):
        for p in (0, 1, X - 1, X):
            coefficients(p)
        MA[0] = diagonal(X - 1, diagonal(0, zero()))
    with scope("startx_1"):
        start_x(1, field_tile(1))

    with scope("coef"):
        @pl.loop(2, X - 1)
        def _(p):
            coefficients(p)

    with scope("diag"):
        width = group_size(X - 2, 6)

        @pl.loop(0, (X - 2) // width)
        def _(g):
            total = zero()
            for i in range(width):
                total = diagonal(1 + g * width + i, total)
            MA[0] = MA[0] + total

    def planes(r, x0, width):
        odd, evn = zero(), zero()
        field, nxt = V[r], V[r + 1]
        for a in tiles:
            rows, up, down = pl.ds(a, T8), pl.ds(a + 1, T8), pl.ds(a - 1, T8)
            own = pl.ds(a - PAD, T8)
            halo = CP[rows, :]
            m, mu, md = field[x0, rows, :], field[x0, up, :], field[x0, down, :]
            v, vu, vd = field[x0 + 1, rows, :], field[x0 + 1, up, :], field[x0 + 1, down, :]
            tv = zp(v)
            acc = F[0, x0, rows, :] * m + F[3, x0, down, :] * md
            acc = acc - F[4, x0, rows, :] * mu - F[6, x0, rows, :] * zp(m)
            accs = F[5, x0, rows, :] * m
            for i in range(width):
                x = x0 + i
                p = x + 1
                n, nu, nd = field[p + 1, rows, :], field[p + 1, up, :], field[p + 1, down, :]
                tn = zp(n)
                f0 = F[0, p, rows, :]
                f2 = F[2, p, rows, :]
                f3, f3d = F[3, p, rows, :], F[3, p, down, :]
                f4, f4d = F[4, p, rows, :], F[4, p, down, :]
                f5, f6 = F[5, p, rows, :], F[6, p, rows, :]
                f7, f7d = F[7, p, rows, :], F[7, p, down, :]
                f8, f8d = F[8, p, rows, :], F[8, p, down, :]
                s = (accs + f2 * v) + (f7d * vd - f8 * vu) - f6 * n
                q = (acc + f0 * n) + (F[1, p, rows, :] * vu + F[1, p, down, :] * vd)
                q = q + (f3 * nu - f4d * nd) + (f2 * tv + f5 * tn)
                q = q + (f7 * zp(vu) - f8d * zp(vd))
                q = q + zm(s) + unpack(halo, x)
                acc = (f0 * v + f3d * vd) - (f4 * vu + f6 * tv)
                accs = f5 * v
                odd = odd + v * q
                w = q * DI[x, own, :]
                evn = evn + w * q
                nxt[p, rows, :] = w
                v, vu, vd, tv = n, nu, nd, tn
        return odd, evn

    def pairs(r, x0, width):
        total = zero()
        field = V[r]
        for a in tiles:
            rows, up = pl.ds(a, T8), pl.ds(a + 1, T8)
            v, vu = field[x0 + 1, rows, :], field[x0 + 1, up, :]
            tv, tvu = zp(v), zp(vu)
            for i in range(width):
                p = x0 + i + 1
                n, nu = field[p + 1, rows, :], field[p + 1, up, :]
                tn, tnu = zp(n), zp(nu)
                a0 = (F[0, p, rows, :] * n + F[1, p, rows, :] * vu) + (F[3, p, rows, :] * nu + F[5, p, rows, :] * tn)
                a0 = a0 + F[7, p, rows, :] * tvu
                a1 = F[2, p, rows, :] * v - F[6, p, rows, :] * n - F[8, p, rows, :] * vu
                total = total + v * a0 + (tv * a1 - (F[4, p, rows, :] * n) * vu)
                v, vu, tv, tvu = n, nu, tn, tnu
        return total

    def along_x(a):
        return pltpu.roll(a, LANES - 2, 1) - pltpu.roll(a, 2, 1)

    def along_y(a):
        return pltpu.roll(a, YE - 1, 0) - pltpu.roll(a, 1, 0)

    sign = jnp.where(even, f32(-1.0), f32(1.0))
    for step in range(ITERS):
        r = step + 1
        last = step + 1 == ITERS
        with scope(f"pack_{r}"):
            pack(r, field_tile(r))
        with scope(f"start_{r}"):
            start_rest(r)
        with scope(f"wait_{r}"):
            wait(r)
        with scope(f"halo_{r}"):
            build_halo(r)
            h = HB[...]
            CP[...] = (PG[0] + HS[0]) * h + sign * (
                PG[1] * along_x(h) + along_x(HS[1] * h) + PG[2] * along_y(h) + along_y(HS[2] * h)
            )
        if last:
            break
        with scope(f"edge_{r}"):
            o0, e0 = planes(r, 0, 1)
            o1, e1 = planes(r, X - 1, 1)
            MA[2 * step + 1] = o0 + o1
            MA[2 * step + 2] = e0 + e1
        with scope(f"startx_{r + 1}"):
            start_x(r + 1, field_tile(r + 1))
        with scope(f"matvec_{r}"):
            width = group_size(X - 2, 6)

            @pl.loop(0, (X - 2) // width)
            def _(g):
                odd, evn = planes(r, 1 + g * width, width)
                MA[2 * step + 1] = MA[2 * step + 1] + odd
                MA[2 * step + 2] = MA[2 * step + 2] + evn

    with scope("pairs"):
        width = group_size(X, 8)
        mine = jnp.logical_and(lane_8 % 2 == 1, jnp.logical_or(lane_8 < 2 * (X - 1), lane_8 == LANES - 1))
        total = zero()
        for a in tiles:
            rows = pl.ds(a, T8)
            total = total + jnp.where(mine, PS[ROUNDS - 1, rows, :] * CP[rows, :], 0.0)
        MA[MOMENTS - 1] = total

        @pl.loop(0, X // width)
        def _(g):
            MA[MOMENTS - 1] = MA[MOMENTS - 1] + pairs(ROUNDS - 1, g * width, width)

    with scope("allreduce"):
        tile = zero()
        for k in range(MOMENTS):
            value = jnp.sum(jnp.sum(MA[k], axis=0, keepdims=True), axis=1, keepdims=True)
            tile = jnp.where(lane_8 == k, value * (2.0 if k == MOMENTS - 1 else 1.0), tile)
        for order, group in enumerate(groups):
            slot = 0
            members = 1
            for i in group:
                slot = slot * sizes[i] + me[i]
                members *= sizes[i]
            RS[order] = tile[0:1]
            copies = []
            for index, t in enumerate(offsets(group)):
                c = pltpu.make_async_remote_copy(
                    src_ref=RS.at[order],
                    dst_ref=RR.at[order, slot],
                    send_sem=ar_send.at[order, index],
                    recv_sem=ar_recv.at[order, index],
                    device_id=partner(t),
                    device_id_type=pl.DeviceIdType.MESH,
                )
                c.start()
                copies.append(c)
            RR[order, slot] = tile[0:1]
            for c in copies:
                c.wait()
            parts = [RR[order, t] for t in range(members)]
            while len(parts) > 1:
                parts = [sum(parts[i + 1 : i + 2], parts[i]) for i in range(0, len(parts), 2)]
            tile = jnp.broadcast_to(parts[0], (T8, LANES))

    n0, n1, n2, n3, n4, n5 = (
        jnp.sum(jnp.where(lane_8 == k, tile, 0.0)[0:1], axis=1, keepdims=True) for k in range(MOMENTS)
    )

    def inverse_of(d):
        return jnp.where(d > 0.0, 1.0 / d, 0.0)

    g00, g01, g02, g12, g22 = n0 - n1, n1 - n2, n2 - n3, n3 - n4, n4 - n5
    i0 = 1.0 / g00
    l1, l2 = g01 * i0, g02 * i0
    i1 = inverse_of(g02 - l1 * g01)
    e = g12 - l2 * g01
    l21 = e * i1
    i2 = inverse_of(g22 - l2 * g02 - l21 * e)
    y1 = n1 - l1 * n0
    y2 = n2 - l2 * n0 - l21 * y1
    c2 = y2 * i2
    c1 = y1 * i1 - l21 * c2
    c0 = n0 * i0 - l1 * c1 - l2 * c2

    with scope("output"):
        @pl.loop(0, X, unroll=4)
        def _(x):
            for a in tiles:
                rows = pl.ds(a, T8)
                out[x, pl.ds(a - PAD, T8), :] = (
                    c0 * V[1][x + 1, rows, :] + c1 * V[2][x + 1, rows, :] + c2 * V[3][x + 1, rows, :]
                )

    for r in range(ROUNDS):
        for d in directions:
            if needed(d, r):
                pl.when(present(d))(lambda d=d, r=r: copy(d, r).wait_send())


def solution(mesh):
    sizes = tuple(mesh.shape[a] for a in AXES)

    def local(labels, conductivity, right_side):
        X, Y, Z = right_side.shape
        YE = Y + 2 * PAD
        f32 = jnp.float32
        vmem = pltpu.VMEM
        return pl.pallas_call(
            functools.partial(kernel, sizes),
            out_shape=jax.ShapeDtypeStruct((X, Y, Z), f32),
            in_specs=[
                pl.BlockSpec(memory_space=pl.ANY),
                pl.BlockSpec(memory_space=pltpu.SMEM),
                pl.BlockSpec(memory_space=pl.ANY),
            ],
            out_specs=pl.BlockSpec(memory_space=pltpu.VMEM),
            scratch_shapes=[
                vmem((X, Y, Z), jnp.int32),
                vmem((X, Y, Z), f32),
                vmem((X + 2, YE, Z), f32),
                vmem((X + 2, YE, Z), f32),
                vmem((X + 2, YE, Z), f32),
                vmem((X + 2, YE, Z), f32),
                vmem((6, X + 2, YE, Z), f32),
                vmem((9, X + 1, YE, Z), f32),
                vmem((X, Y, Z), f32),
                vmem((ROUNDS, YE, Z), f32),
                vmem((ROUNDS, 2, YE, Z), f32),
                vmem((ROUNDS, 8, Z), f32),
                vmem((ROUNDS, 4, 8, Z), f32),
                vmem((YE, Z), f32),
                vmem((3, YE, Z), f32),
                vmem((3, YE, Z), f32),
                vmem((YE, Z), f32),
                vmem((MOMENTS, 8, Z), f32),
                vmem((2, 1, Z), f32),
                vmem((2, 32, 1, Z), f32),
                pltpu.SemaphoreType.DMA((ROUNDS, 18)),
                pltpu.SemaphoreType.DMA((ROUNDS, 18)),
                pltpu.SemaphoreType.DMA((2, 32)),
                pltpu.SemaphoreType.DMA((2, 32)),
                pltpu.SemaphoreType.DMA((2,)),
            ],
            compiler_params=pltpu.CompilerParams(
                collective_id=0, has_side_effects=True, vmem_limit_bytes=60 * 1024 * 1024
            ),
        )(labels, conductivity, right_side)

    return jax.shard_map(
        local,
        mesh=mesh,
        in_specs=(P("gx", "gy", "gz"), P(), P("gx", "gy", "gz")),
        out_specs=P("gx", "gy", "gz"),
        check_vma=False,
    )
```

time: 53.4 us -> 40.8 us (0.76)
  Pallas kernels: 50.8 us -> 38.3 us
    pallas_call x1, Pallas kernels: 50.8 us -> 38.3 us  [local(): pl.pallas_call(functools.partial(kernel, sizes), out_shape=jax.ShapeDtype...]
where the time goes in v1:
time: 40.8 us; the launch traced here: 40.6 us
  Pallas kernels  38.3 us (94%)
  local copies, waits for them, and re-layouts  2.31 us (6%)
    pallas_call x1, Pallas kernels, local(): pl.pallas_call(functools.partial(kernel, sizes), out_shape=jax.ShapeDtype...  38.3 us
    unnamed x1, local copies, waits for them, and re-layouts  2.31 us

profile of v1, /device:TPU:0, one launch (start us, length us, event | category | flops | bytes accessed | tf_op | source)
XLA Modules:
  0.0 40.6 jit_solution(5857231025200816335)
XLA Ops:
  0.0 38.3 %shard_map.37 = f32[32,64,128]{2,1,0:T(8,128)} custom-call(s32[32,64,128]{2,1,0:T(8,128)} %lab_hbm.1, f32[7,8]{1,0:T(8,128)} %cond.1, f32[32,64,128]{2,1,0:T(8,128)} %rhs_hbm.1), custom_call_target="tpu_custom_call" | custom-call | tf_op jit(solution)/shard_map/pallas_call | solution.py:545
  38.3 2.3 %copy.5 = f32[32,64,128]{2,1,0:T(8,128)} copy(f32[32,64,128]{2,1,0:T(8,128)} %shard_map.37) | data formatting | bytes 2097152

commit v2 on v1

--- a/solution.py
+++ b/solution.py
@@ -21,16 +21,21 @@
     return max(u for u in range(1, most + 1) if n % u == 0)
 
 
+def groups_of(sizes):
+    return [(0, 1, 2)] if math.prod(sizes) <= 32 else [(0, 1), (2,)]
+
+
 def kernel(
-    sizes, lab_hbm, cond, rhs_hbm, out, lab, rhs, V0, V1, V2, V3, S, F, DI, PS, PR, ES, ER, HB, HS, PG, CP, MA, RS,
-    RR, send_sem, recv_sem, ar_send, ar_recv, in_sem,
+    sizes, lab_hbm, cond_hbm, rhs_hbm, W, C, lab, cond, rhs, V0, V1, V2, V3, S, F, DI, PS, PZ, PR, ZR, ES, ER, HB, HS, PG, CP,
+    MA, RS, RR, send_sem, recv_sem, ar_send, ar_recv, in_sem,
 ):
     V = (V0, V1, V2, V3)
     X, Y, Z = rhs.shape
     lab_copy = pltpu.make_async_copy(lab_hbm, lab, in_sem.at[0])
     lab_copy.start()
+    cond_copy = pltpu.make_async_copy(cond_hbm, cond, in_sem.at[2])
+    cond_copy.start()
     rhs_copy = pltpu.make_async_copy(rhs_hbm, rhs, in_sem.at[1])
-    rhs_copy.start()
     YE = Y + 2 * PAD
     TOP = PAD + Y
     KT = Y // T8
@@ -73,8 +78,10 @@
             fx, tx = (X, 0) if dx > 0 else (1, X + 1)
             return V[r].at[fx, rows_from], V[r].at[tx, rows_to]
         side = 0 if dz > 0 else 1
+        if dx == 0 and dy == 0:
+            return PZ.at[r, side], ZR.at[r, side]
         if dx == 0:
-            return PS.at[r, rows_from], PR.at[r, side, rows_to]
+            return PS.at[r, rows_from], PR.at[r, side, 0 if dy > 0 else 1]
         slot = (0 if dx > 0 else 2) + side
         return ES.at[r], ER.at[r, slot]
 
@@ -84,13 +91,13 @@
         return pltpu.make_async_remote_copy(
             src_ref=src,
             dst_ref=dst,
-            send_sem=send_sem.at[r, m],
-            recv_sem=recv_sem.at[r, m],
+            send_sem=send_sem.at[r % 2, m],
+            recv_sem=recv_sem.at[r % 2, m],
             device_id=tuple(a + t for a, t in zip(me, d)),
             device_id_type=pl.DeviceIdType.MESH,
         )
 
-    groups = [(0, 1, 2)] if math.prod(sizes) <= 32 else [(0, 1), (2,)]
+    groups = groups_of(sizes)
     near = len(groups) == 1 and max(sizes) <= ROUNDS and sum(n - 1 for n in sizes) <= 2 * ROUNDS - 1
 
     def offsets(group):
@@ -153,15 +160,6 @@
     inner = lane_8 < LANES - 1
     tiles = [PAD + T8 * k for k in range(KT)]
 
-    scale = (0.5, 0.5, 0.5, 0.25, 0.25, 0.25, 1.0)
-    count = cond.shape[1]
-    tables = []
-    for c in range(7):
-        table = jnp.zeros((T8, LANES), f32)
-        for k in range(count):
-            table = jnp.where(row_8 == k, cond[c, k] * scale[c], table)
-        tables.append(table)
-
     def look(c, index):
         return jnp.take_along_axis(tables[c], index, axis=0, mode="promise_in_bounds")
 
@@ -169,6 +167,10 @@
         index = jnp.maximum(values.astype(jnp.int32) - 1, 0)
         hit = values > 0.0
         return [jnp.where(hit, look(c, index), 0.0) for c in components]
+
+    half = LANES // 2
+    offs = (0, 1, half, half + 1)
+    slots_of = [jnp.logical_and(lane_8 % 2 == off % 2, (lane_8 < half) == (off < half)) for off in offs]
 
     def send(d, r):
         if d in directions and needed(d, r):
@@ -187,22 +189,51 @@
                 send(d, r)
 
     def start_rest(r):
-        for d in directions:
+        for d in sorted(directions, key=lambda d: (-abs(d[2]), abs(d[1]))):
             if not d[0]:
                 send(d, r)
 
+    def wait_sent(r):
+        for d in directions:
+            if needed(d, r):
+                pl.when(present(d))(lambda d=d: copy(d, r).wait_send())
+
     def wait(r):
+        if r:
+            wait_sent(r - 1)
         for d in directions:
             if needed(d, r):
                 back = tuple(-t for t in d)
                 pl.when(present(back))(lambda d=d: copy(d, r).wait_recv())
 
+    def spread(r):
+        for side in range(2):
+            if side == 0 and r == ROUNDS - 1:
+                continue
+            for t in range(KT // 4):
+                tile = None
+                for j, off in enumerate(offs):
+                    part = PS[r, pl.ds(PAD + T8 * (4 * t + j), T8), :]
+                    part = pltpu.roll(part, (off + 1 - side) % LANES, 1) if off + 1 - side else part
+                    tile = part if tile is None else jnp.where(slots_of[j], part, tile)
+                PZ[r, side, pl.ds(T8 * t, T8), :] = tile
+
     def build_halo(r):
-        low = pltpu.roll(PR[r, 0], 1, 1)
-        high = pltpu.roll(PR[r, 1], LANES - 1, 1)
-        valid = jnp.logical_or(lane_e <= 2 * (X - 1), lane_e == LANES - 1)
+        valid = jnp.logical_or(lane_8 <= 2 * (X - 1), lane_8 == LANES - 1)
+        even = lane_8 % 2 == 0
         last = r == ROUNDS - 1
-        HB[...] = jnp.where(valid, jnp.where(even, 0.0 if last else low, high), 0.0)
+
+        def join(low, high):
+            return jnp.where(valid, jnp.where(even, 0.0 if last else low, high), 0.0)
+
+        for i, a in enumerate((0, TOP)):
+            low = None if last else pltpu.roll(PR[r, 0, i], 1, 1)
+            HB[pl.ds(a, T8), :] = join(low, pltpu.roll(PR[r, 1, i], LANES - 1, 1))
+        for k in range(KT):
+            t, off = pl.ds(T8 * (k // 4), T8), offs[k % 4]
+            low = None if last else pltpu.roll(ZR[r, 0, t, :], (LANES - off) % LANES, 1)
+            high = pltpu.roll(ZR[r, 1, t, :], LANES - 1 - off, 1)
+            HB[pl.ds(PAD + T8 * k, T8), :] = join(low, high)
         targets = (((LANES - 2), 3), ((LANES - 3), 2), (2 * X, 1), (2 * X - 1, 0))
         slots = (1, 3) if last else (0, 1, 2, 3)
         got = {slot: ER[r, slot] for slot in slots}
@@ -233,6 +264,7 @@
                 here = jnp.logical_and(lane_8 >= 2 * x - 1, inner)
                 tile = jnp.where(here, pltpu.roll(plane(x, k), 2 * x, 1), tile)
             PS[r, pl.ds(PAD + T8 * k, T8), :] = tile
+        spread(r)
 
     def label_tile(x, k):
         return (lab[x, pl.ds(T8 * k, T8), :] + 1).astype(f32)
@@ -242,6 +274,7 @@
 
     with scope("labwait"):
         lab_copy.wait()
+        rhs_copy.start()
 
     with scope("conv"):
         for x in (0, X - 1):
@@ -252,13 +285,25 @@
             for k in (0, KT - 1):
                 V[0][x + 1, pl.ds(PAD + T8 * k, T8), :] = label_tile(x, k)
 
-    with scope("pack0"):
-        pack(0, label_tile)
     with scope("barrier"):
         pl.semaphore_wait(barrier, greeted)
     with scope("start0"):
         start_x(0, label_tile)
+    with scope("pack0"):
+        pack(0, label_tile)
+    with scope("start_0"):
         start_rest(0)
+
+    cond_copy.wait()
+    scale = (0.5, 0.5, 0.5, 0.25, 0.25, 0.25, 1.0)
+    count = cond.shape[1]
+    tables = []
+    for c in range(7):
+        table = jnp.zeros((T8, LANES), f32)
+        for k in range(count):
+            table = jnp.where(row_8 == k, cond[c, k] * scale[c], table)
+        tables.append(table)
+
 
     with scope("sigma_own"):
         @pl.loop(0, X, unroll=4)
@@ -292,7 +337,7 @@
                 HS[i, rows, :] = s
             for i, s in enumerate(look_known(PS[0, rows, :], (2, 4, 5))):
                 PG[i, rows, :] = s
-        CP[...] = PG[0] + HS[0]
+        CP[...] = HS[0]
         rhs_copy.wait()
 
     def coefficients(p):
@@ -318,12 +363,14 @@
     def diagonal(x, total):
         p = x + 1
         for a in tiles:
-            rows, down = pl.ds(a, T8), pl.ds(a - 1, T8)
+            rows, up, down = pl.ds(a, T8), pl.ds(a + 1, T8), pl.ds(a - 1, T8)
             own = pl.ds(a - PAD, T8)
-            f2 = F[2, p, rows, :]
-            diag = look(6, lab[x, own, :]) + F[0, p, rows, :] + F[0, p - 1, rows, :]
-            diag = diag + F[1, p, rows, :] + F[1, p, down, :]
-            diag = diag + (f2 + zm(f2)) + unpack(CP[rows, :], x)
+            s2 = S[2, p, rows, :]
+            face = pltpu.roll(CP[rows, :], lax.rem(LANES - 2 * x, LANES), 1)
+            diag = look(6, lab[x, own, :]) + 2.0 * ((S[0, p, rows, :] + S[1, p, rows, :]) + s2)
+            diag = diag + (S[0, p - 1, rows, :] + S[0, p + 1, rows, :])
+            diag = diag + (S[1, p, down, :] + S[1, p, up, :])
+            diag = diag + (jnp.where(lane_8 == 0, face, zm(s2)) + jnp.where(inner, zp(s2), face))
             inverse = 1.0 / diag
             DI[x, own, :] = inverse
             r0 = rhs[x, own, :]
@@ -335,18 +382,10 @@
     def zero():
         return jnp.zeros((T8, LANES), f32)
 
-    with scope("coef_x"):
-        for p in (0, 1, X - 1, X):
-            coefficients(p)
+    with scope("diag_x"):
         MA[0] = diagonal(X - 1, diagonal(0, zero()))
     with scope("startx_1"):
         start_x(1, field_tile(1))
-
-    with scope("coef"):
-        @pl.loop(2, X - 1)
-        def _(p):
-            coefficients(p)
-
     with scope("diag"):
         width = group_size(X - 2, 6)
 
@@ -356,6 +395,18 @@
             for i in range(width):
                 total = diagonal(1 + g * width + i, total)
             MA[0] = MA[0] + total
+
+    with scope("pack_1"):
+        pack(1, field_tile(1))
+    with scope("start_1"):
+        start_rest(1)
+    with scope("coef"):
+        width = group_size(X + 1, 4)
+
+        @pl.loop(0, (X + 1) // width)
+        def _(g):
+            for i in range(width):
+                coefficients(g * width + i)
 
     def planes(r, x0, width):
         odd, evn = zero(), zero()
@@ -424,18 +475,27 @@
     for step in range(ITERS):
         r = step + 1
         last = step + 1 == ITERS
-        with scope(f"pack_{r}"):
-            pack(r, field_tile(r))
-        with scope(f"start_{r}"):
-            start_rest(r)
+        if step:
+            with scope(f"pack_{r}"):
+                pack(r, field_tile(r))
+            with scope(f"start_{r}"):
+                start_rest(r)
+        if last:
+            with scope("early_sums"):
+                tile = zero()
+                for k in range(MOMENTS - 1):
+                    value = jnp.sum(jnp.sum(MA[k], axis=0, keepdims=True), axis=1, keepdims=True)
+                    tile = jnp.where(lane_8 == k, value, tile)
+                CP[pl.ds(0, T8), :] = tile
         with scope(f"wait_{r}"):
             wait(r)
         with scope(f"halo_{r}"):
             build_halo(r)
             h = HB[...]
-            CP[...] = (PG[0] + HS[0]) * h + sign * (
+            full = (PG[0] + HS[0]) * h + sign * (
                 PG[1] * along_x(h) + along_x(HS[1] * h) + PG[2] * along_y(h) + along_y(HS[2] * h)
             )
+            CP[pl.ds(PAD, Y), :] = full[PAD:TOP]
         if last:
             break
         with scope(f"edge_{r}"):
@@ -467,11 +527,18 @@
         def _(g):
             MA[MOMENTS - 1] = MA[MOMENTS - 1] + pairs(ROUNDS - 1, g * width, width)
 
+    def leave():
+        wait_sent(ROUNDS - 1)
+
+        @pl.loop(0, X, unroll=4)
+        def _(x):
+            for i in range(ITERS):
+                for k in range(KT):
+                    W[i, x, pl.ds(T8 * k, T8), :] = V[i + 1][x + 1, pl.ds(PAD + T8 * k, T8), :]
+
     with scope("allreduce"):
-        tile = zero()
-        for k in range(MOMENTS):
-            value = jnp.sum(jnp.sum(MA[k], axis=0, keepdims=True), axis=1, keepdims=True)
-            tile = jnp.where(lane_8 == k, value * (2.0 if k == MOMENTS - 1 else 1.0), tile)
+        value = jnp.sum(jnp.sum(MA[MOMENTS - 1], axis=0, keepdims=True), axis=1, keepdims=True)
+        tile = jnp.where(lane_8 == MOMENTS - 1, 2.0 * value, CP[pl.ds(0, T8), :])
         for order, group in enumerate(groups):
             slot = 0
             members = 1
@@ -479,21 +546,22 @@
                 slot = slot * sizes[i] + me[i]
                 members *= sizes[i]
             RS[order] = tile[0:1]
-            copies = []
-            for index, t in enumerate(offsets(group)):
-                c = pltpu.make_async_remote_copy(
+            others = offsets(group)
+            for t in others:
+                pltpu.make_async_remote_copy(
                     src_ref=RS.at[order],
                     dst_ref=RR.at[order, slot],
-                    send_sem=ar_send.at[order, index],
-                    recv_sem=ar_recv.at[order, index],
+                    send_sem=ar_send.at[order],
+                    recv_sem=ar_recv.at[order],
                     device_id=partner(t),
                     device_id_type=pl.DeviceIdType.MESH,
-                )
-                c.start()
-                copies.append(c)
+                ).start()
             RR[order, slot] = tile[0:1]
-            for c in copies:
-                c.wait()
+            if order == 0:
+                leave()
+            sent = RR.at[order, pl.ds(0, len(others))]
+            pltpu.make_async_copy(sent, sent, ar_send.at[order]).wait()
+            pltpu.make_async_copy(sent, sent, ar_recv.at[order]).wait()
             parts = [RR[order, t] for t in range(members)]
             while len(parts) > 1:
                 parts = [sum(parts[i + 1 : i + 2], parts[i]) for i in range(0, len(parts), 2)]
@@ -519,19 +587,29 @@
     c1 = y1 * i1 - l21 * c2
     c0 = n0 * i0 - l1 * c1 - l2 * c2
 
-    with scope("output"):
-        @pl.loop(0, X, unroll=4)
+    for i, c in enumerate((c0, c1, c2)):
+        C[pl.ds(i, 1), :] = jnp.broadcast_to(c, (1, LANES))
+
+
+def combine(W, C, out, part, sem):
+    X, Y, Z = out.shape
+    rows = C[...]
+    c = [jnp.broadcast_to(rows[i : i + 1], (T8, Z)) for i in range(ITERS)]
+    pieces = sem.shape[0]
+    width = X // pieces
+    copies = []
+    for g in range(pieces):
+        @pl.loop(g * width, (g + 1) * width, unroll=4)
         def _(x):
-            for a in tiles:
-                rows = pl.ds(a, T8)
-                out[x, pl.ds(a - PAD, T8), :] = (
-                    c0 * V[1][x + 1, rows, :] + c1 * V[2][x + 1, rows, :] + c2 * V[3][x + 1, rows, :]
-                )
-
-    for r in range(ROUNDS):
-        for d in directions:
-            if needed(d, r):
-                pl.when(present(d))(lambda d=d, r=r: copy(d, r).wait_send())
+            for k in range(Y // T8):
+                own = pl.ds(T8 * k, T8)
+                part[x, own, :] = (c[0] * W[0, x, own, :] + c[1] * W[1, x, own, :]) + c[2] * W[2, x, own, :]
+
+        block = pl.ds(g * width, width)
+        copies.append(pltpu.make_async_copy(part.at[block], out.at[block], sem.at[g]))
+        copies[-1].start()
+    for piece in copies:
+        piece.wait()
 
 
 def solution(mesh):
@@ -542,17 +620,19 @@
         YE = Y + 2 * PAD
         f32 = jnp.float32
         vmem = pltpu.VMEM
-        return pl.pallas_call(
+        orders = len(groups_of(sizes))
+        fields, factors = pl.pallas_call(
             functools.partial(kernel, sizes),
-            out_shape=jax.ShapeDtypeStruct((X, Y, Z), f32),
+            out_shape=(vmem((ITERS, X, Y, Z), f32), vmem((T8, Z), f32)),
             in_specs=[
                 pl.BlockSpec(memory_space=pl.ANY),
-                pl.BlockSpec(memory_space=pltpu.SMEM),
+                pl.BlockSpec(memory_space=pl.ANY),
                 pl.BlockSpec(memory_space=pl.ANY),
             ],
-            out_specs=pl.BlockSpec(memory_space=pltpu.VMEM),
+            out_specs=[pl.BlockSpec(memory_space=vmem)] * 2,
             scratch_shapes=[
                 vmem((X, Y, Z), jnp.int32),
+                pltpu.SMEM(conductivity.shape, f32),
                 vmem((X, Y, Z), f32),
                 vmem((X + 2, YE, Z), f32),
                 vmem((X + 2, YE, Z), f32),
@@ -562,7 +642,9 @@
                 vmem((9, X + 1, YE, Z), f32),
                 vmem((X, Y, Z), f32),
                 vmem((ROUNDS, YE, Z), f32),
-                vmem((ROUNDS, 2, YE, Z), f32),
+                vmem((ROUNDS, 2, Y // 4, Z), f32),
+                vmem((ROUNDS, 2, 2, T8, Z), f32),
+                vmem((ROUNDS, 2, Y // 4, Z), f32),
                 vmem((ROUNDS, 8, Z), f32),
                 vmem((ROUNDS, 4, 8, Z), f32),
                 vmem((YE, Z), f32),
@@ -572,16 +654,24 @@
                 vmem((MOMENTS, 8, Z), f32),
                 vmem((2, 1, Z), f32),
                 vmem((2, 32, 1, Z), f32),
-                pltpu.SemaphoreType.DMA((ROUNDS, 18)),
-                pltpu.SemaphoreType.DMA((ROUNDS, 18)),
-                pltpu.SemaphoreType.DMA((2, 32)),
-                pltpu.SemaphoreType.DMA((2, 32)),
-                pltpu.SemaphoreType.DMA((2,)),
+                pltpu.SemaphoreType.DMA((2, 18)),
+                pltpu.SemaphoreType.DMA((2, 18)),
+                pltpu.SemaphoreType.DMA((orders,)),
+                pltpu.SemaphoreType.DMA((orders,)),
+                pltpu.SemaphoreType.DMA((3,)),
             ],
             compiler_params=pltpu.CompilerParams(
                 collective_id=0, has_side_effects=True, vmem_limit_bytes=60 * 1024 * 1024
             ),
         )(labels, conductivity, right_side)
+        return pl.pallas_call(
+            combine,
+            out_shape=jax.ShapeDtypeStruct((X, Y, Z), f32),
+            in_specs=[pl.BlockSpec(memory_space=vmem)] * 2,
+            out_specs=pl.BlockSpec(memory_space=pl.ANY),
+            scratch_shapes=[vmem((X, Y, Z), f32), pltpu.SemaphoreType.DMA((group_size(X, 4),))],
+            compiler_params=pltpu.CompilerParams(vmem_limit_bytes=8 * 1024 * 1024),
+        )(fields, factors)
 
     return jax.shard_map(
         local,

time: 40.8 us -> 31.8 us (0.78)
  Pallas kernels: 38.3 us -> 31.7 us
  local copies, waits for them, and re-layouts: 2.31 us -> 0 us
    pallas_call x1 -> x2, Pallas kernels: 38.3 us -> 31.7 us  [the longest x1 30.6 us: local(): pl.pallas_call(functools.partial(kernel, sizes), out_shape=(vmem((ITERS,...]
    unnamed x1 -> x0, local copies, waits for them, and re-layouts: 2.31 us -> none
where the time goes in v2:
time: 31.8 us; the launch traced here: 31.7 us
  Pallas kernels  31.7 us (100%)
    pallas_call x1, Pallas kernels, local(): pl.pallas_call(functools.partial(kernel, sizes), out_shape=(vmem((ITERS,...  30.6 us
    pallas_call x1, Pallas kernels, local(): pl.pallas_call(combine, out_shape=jax.ShapeDtypeStruct((X, Y, Z), f32), i...  1.05 us

profile of v2, /device:TPU:0, one launch (start us, length us, event | category | flops | bytes accessed | tf_op | source)
XLA Modules:
  0.0 31.7 jit_solution(4055302559467057078)
XLA Ops:
  0.0 30.6 %shard_map.37 = (f32[3,32,64,128]{3,2,1,0:T(8,128)S(1)}, f32[8,128]{1,0:T(8,128)S(1)}) custom-call(s32[32,64,128]{2,1,0:T(8,128)} %lab_hbm.1, f32[7,8]{1,0:T(8,128)} %cond_hbm.1, f32[32,64,128]{2,1,0:T(8,128)} %rhs_hbm.1), custom_call_target="tpu_custom_call" | custom-call | tf_op jit(solution)/shard_map/pallas_call | solution.py:624
  30.6 1.0 %shard_map.38 = f32[32,64,128]{2,1,0:T(8,128)} custom-call(f32[3,32,64,128]{3,2,1,0:T(8,128)S(1)} %get-tuple-element.7.W, f32[8,128]{1,0:T(8,128)S(1)} %get-tuple-element.8.C), custom_call_target="tpu_custom_call" | custom-call | tf_op jit(solution)/shard_map/pallas_call | solution.py:667

commit v3 on v2

--- a/solution.py
+++ b/solution.py
@@ -27,11 +27,16 @@
 
 def kernel(
     sizes, lab_hbm, cond_hbm, rhs_hbm, W, C, lab, cond, rhs, V0, V1, V2, V3, S, F, DI, PS, PZ, PR, ZR, ES, ER, HB, HS, PG, CP,
-    MA, RS, RR, send_sem, recv_sem, ar_send, ar_recv, in_sem,
+    DP, MA, RS, RR, send_sem, recv_sem, ar_send, ar_recv, in_sem,
 ):
     V = (V0, V1, V2, V3)
     X, Y, Z = rhs.shape
-    lab_copy = pltpu.make_async_copy(lab_hbm, lab, in_sem.at[0])
+    end_copies = []
+    for i, x in enumerate((0, X - 1)):
+        end_copies.append(pltpu.make_async_copy(lab_hbm.at[x], lab.at[x], in_sem.at[3 + i]))
+        end_copies[-1].start()
+    inside = pl.ds(1, X - 2)
+    lab_copy = pltpu.make_async_copy(lab_hbm.at[inside], lab.at[inside], in_sem.at[0])
     lab_copy.start()
     cond_copy = pltpu.make_async_copy(cond_hbm, cond, in_sem.at[2])
     cond_copy.start()
@@ -70,8 +75,8 @@
 
     def places(d, r):
         dx, dy, dz = d
-        rows_from = pl.ds(PAD, Y) if dy == 0 else (pl.ds(TOP - 8, 8) if dy > 0 else pl.ds(PAD, 8))
-        rows_to = pl.ds(PAD, Y) if dy == 0 else (pl.ds(0, 8) if dy > 0 else pl.ds(TOP, 8))
+        rows_from = pl.ds(PAD, Y) if dy == 0 else (pl.ds(TOP - 1, 1) if dy > 0 else pl.ds(PAD, 1))
+        rows_to = pl.ds(PAD, Y) if dy == 0 else (pl.ds(PAD - 1, 1) if dy > 0 else pl.ds(TOP, 1))
         if dz == 0:
             if dx == 0:
                 return V[r].at[pl.ds(1, X), rows_from], V[r].at[pl.ds(1, X), rows_to]
@@ -81,7 +86,7 @@
         if dx == 0 and dy == 0:
             return PZ.at[r, side], ZR.at[r, side]
         if dx == 0:
-            return PS.at[r, rows_from], PR.at[r, side, 0 if dy > 0 else 1]
+            return PS.at[r, rows_from], PR.at[r, side, 0 if dy > 0 else 1, pl.ds(PAD - 1 if dy > 0 else 0, 1)]
         slot = (0 if dx > 0 else 2) + side
         return ES.at[r], ER.at[r, slot]
 
@@ -150,6 +155,13 @@
     for r in range(ROUNDS):
         for a in (0, TOP):
             PS[r, pl.ds(a, PAD), :] = jnp.zeros((PAD, LANES), f32)
+    for r in range(ROUNDS):
+        for side in range(2):
+            PR[r, side, 0, pl.ds(0, PAD - 1), :] = jnp.zeros((PAD - 1, LANES), f32)
+            PR[r, side, 1, pl.ds(1, PAD - 1), :] = jnp.zeros((PAD - 1, LANES), f32)
+    for x in range(X + 2):
+        V[0][x, pl.ds(0, PAD - 1), :] = jnp.zeros((PAD - 1, LANES), f32)
+        V[0][x, pl.ds(TOP + 1, PAD - 1), :] = jnp.zeros((PAD - 1, LANES), f32)
     MA[...] = jnp.zeros(MA.shape, f32)
 
     lane_e = lax.broadcasted_iota(jnp.int32, (YE, LANES), 1)
@@ -184,12 +196,12 @@
                 part = plane(x, k)
                 tile = jnp.where(lane_8 == to, pltpu.roll(part, (to - at) % LANES, 1), tile)
         ES[r] = tile
-        for d in directions:
+        for d in sorted(directions, key=lambda d: (-abs(d[2]), -abs(d[1]))):
             if d[0]:
                 send(d, r)
 
     def start_rest(r):
-        for d in sorted(directions, key=lambda d: (-abs(d[2]), abs(d[1]))):
+        for d in sorted(directions, key=lambda d: (-abs(d[2]), -abs(d[1]))):
             if not d[0]:
                 send(d, r)
 
@@ -257,14 +269,16 @@
     def unpack(part, x):
         return jnp.where(ends, pltpu.roll(part, lax.rem(LANES - 2 * x, LANES), 1), 0.0)
 
+    def packed(plane, k, first, last):
+        tile = None
+        for x in range(first, last):
+            part = pltpu.roll(plane(x, k), 2 * x, 1) if x else plane(x, k)
+            tile = part if tile is None else jnp.where(jnp.logical_and(lane_8 >= 2 * x - 1, inner), part, tile)
+        return tile
+
     def pack(r, plane):
         for k in range(KT):
-            tile = plane(0, k)
-            for x in range(1, X):
-                here = jnp.logical_and(lane_8 >= 2 * x - 1, inner)
-                tile = jnp.where(here, pltpu.roll(plane(x, k), 2 * x, 1), tile)
-            PS[r, pl.ds(PAD + T8 * k, T8), :] = tile
-        spread(r)
+            PS[r, pl.ds(PAD + T8 * k, T8), :] = packed(plane, k, 0, X)
 
     def label_tile(x, k):
         return (lab[x, pl.ds(T8 * k, T8), :] + 1).astype(f32)
@@ -272,25 +286,26 @@
     def field_tile(r):
         return lambda x, k: V[r][x + 1, pl.ds(PAD + T8 * k, T8), :]
 
-    with scope("labwait"):
-        lab_copy.wait()
-        rhs_copy.start()
-
+    with scope("endwait"):
+        for end_copy in end_copies:
+            end_copy.wait()
     with scope("conv"):
         for x in (0, X - 1):
             for k in range(KT):
                 V[0][x + 1, pl.ds(PAD + T8 * k, T8), :] = label_tile(x, k)
-
-        for x in range(1, X - 1):
-            for k in (0, KT - 1):
-                V[0][x + 1, pl.ds(PAD + T8 * k, T8), :] = label_tile(x, k)
-
     with scope("barrier"):
         pl.semaphore_wait(barrier, greeted)
     with scope("start0"):
         start_x(0, label_tile)
+    with scope("labwait"):
+        lab_copy.wait()
+        rhs_copy.start()
     with scope("pack0"):
+        for x in range(1, X - 1):
+            for k in (0, KT - 1):
+                V[0][x + 1, pl.ds(PAD + T8 * k, T8), :] = label_tile(x, k)
         pack(0, label_tile)
+        spread(0)
     with scope("start_0"):
         start_rest(0)
 
@@ -313,52 +328,57 @@
                 for c in range(6):
                     S[c, x + 1, pl.ds(a, T8), :] = look(c, index)
 
+    def coefficients(p, where, inside=True):
+        for a in where:
+            rows, up = pl.ds(a, T8), pl.ds(a + 1, T8)
+            s3, s3u = S[3, p, rows, :], S[3, p, up, :]
+            t3, t3u = S[3, p + 1, rows, :], S[3, p + 1, up, :]
+            F[3, p, rows, :] = s3 + t3u
+            F[4, p, rows, :] = t3 + s3u
+            if inside:
+                s5, s5u = S[5, p, rows, :], S[5, p, up, :]
+                F[1, p, rows, :] = S[1, p, rows, :] + S[1, p, up, :]
+                F[7, p, rows, :] = jnp.where(inner, s5 + zp(s5u), 0.0)
+                F[8, p, rows, :] = jnp.where(inner, s5u + zp(s5), 0.0)
+            if a:
+                s4, t4 = S[4, p, rows, :], S[4, p + 1, rows, :]
+                F[0, p, rows, :] = S[0, p, rows, :] + S[0, p + 1, rows, :]
+                F[5, p, rows, :] = jnp.where(inner, s4 + zp(t4), 0.0)
+                F[6, p, rows, :] = jnp.where(inner, t4 + zp(s4), 0.0)
+                if inside:
+                    s2 = S[2, p, rows, :]
+                    F[2, p, rows, :] = jnp.where(inner, s2 + zp(s2), 0.0)
+
+    with scope("coef_in"):
+        width = group_size(X - 2, 3)
+
+        @pl.loop(0, (X - 2) // width)
+        def _(g):
+            for i in range(width):
+                coefficients(1 + g * width + i, tiles[:-1])
+        coefficients(X - 1, tiles[:-1])
+
     with scope("wait0"):
         wait(0)
 
+    halo_tiles = [pl.ds(a, T8) for a in range(0, YE, T8)]
+
+    def sigma_halo(x, rows, components):
+        for c, s in zip(components, look_known(V[0][x, rows, :], components)):
+            S[c, x, rows, :] = s
+
     with scope("sigma_halo"):
+        build_halo(0)
+        for rows in halo_tiles:
+            (HS[0, rows, :],) = look_known(HB[rows, :], (2,))
+        CP[...] = HS[0]
         for x in (0, X + 1):
-            for a in range(0, YE, T8):
-                rows = pl.ds(a, T8)
-                for c, s in enumerate(look_known(V[0][x, rows, :], range(6))):
-                    S[c, x, rows, :] = s
-
-        @pl.loop(1, X + 1, unroll=4)
-        def _(x):
+            for a in tiles:
+                sigma_halo(x, pl.ds(a, T8), (0,))
+        for x in range(1, X + 1):
             for a in (0, TOP):
-                rows = pl.ds(a, T8)
-                for c, s in enumerate(look_known(V[0][x, rows, :], range(6))):
-                    S[c, x, rows, :] = s
-
-        build_halo(0)
-        for a in range(0, YE, T8):
-            rows = pl.ds(a, T8)
-            for i, s in enumerate(look_known(HB[rows, :], (2, 4, 5))):
-                HS[i, rows, :] = s
-            for i, s in enumerate(look_known(PS[0, rows, :], (2, 4, 5))):
-                PG[i, rows, :] = s
-        CP[...] = HS[0]
+                sigma_halo(x, pl.ds(a, T8), (1,))
         rhs_copy.wait()
-
-    def coefficients(p):
-        for a in [0] + tiles:
-            rows, up = pl.ds(a, T8), pl.ds(a + 1, T8)
-            s1, s1u = S[1, p, rows, :], S[1, p, up, :]
-            s3, s3u = S[3, p, rows, :], S[3, p, up, :]
-            t3, t3u = S[3, p + 1, rows, :], S[3, p + 1, up, :]
-            s5, s5u = S[5, p, rows, :], S[5, p, up, :]
-            F[1, p, rows, :] = s1 + s1u
-            F[3, p, rows, :] = s3 + t3u
-            F[4, p, rows, :] = t3 + s3u
-            F[7, p, rows, :] = jnp.where(inner, s5 + zp(s5u), 0.0)
-            F[8, p, rows, :] = jnp.where(inner, s5u + zp(s5), 0.0)
-            if a:
-                s2 = S[2, p, rows, :]
-                s4, t4 = S[4, p, rows, :], S[4, p + 1, rows, :]
-                F[0, p, rows, :] = S[0, p, rows, :] + S[0, p + 1, rows, :]
-                F[2, p, rows, :] = jnp.where(inner, s2 + zp(s2), 0.0)
-                F[5, p, rows, :] = jnp.where(inner, s4 + zp(t4), 0.0)
-                F[6, p, rows, :] = jnp.where(inner, t4 + zp(s4), 0.0)
 
     def diagonal(x, total):
         p = x + 1
@@ -398,23 +418,40 @@
 
     with scope("pack_1"):
         pack(1, field_tile(1))
+        spread(1)
     with scope("start_1"):
         start_rest(1)
     with scope("coef"):
-        width = group_size(X + 1, 4)
-
-        @pl.loop(0, (X + 1) // width)
+        for rows in halo_tiles:
+            for i, s in enumerate(look_known(HB[rows, :], (4, 5))):
+                HS[i + 1, rows, :] = s
+            for i, s in enumerate(look_known(PS[0, rows, :], (2, 4, 5))):
+                PG[i, rows, :] = s
+            for x in (0, X + 1):
+                sigma_halo(x, rows, (3, 4))
+
+        @pl.loop(1, X + 1, unroll=4)
+        def _(x):
+            for a in (0, TOP):
+                sigma_halo(x, pl.ds(a, T8), (3, 5))
+
+        coefficients(0, [0] + tiles, False)
+        coefficients(X, [0] + tiles)
+        coefficients(X - 1, (0, TOP - T8))
+        width = group_size(X - 2, 10)
+
+        @pl.loop(0, (X - 2) // width)
         def _(g):
             for i in range(width):
-                coefficients(g * width + i)
-
-    def planes(r, x0, width):
+                coefficients(1 + g * width + i, (0, TOP - T8))
+
+    def planes(r, x0, width, where, ready=True):
         odd, evn = zero(), zero()
         field, nxt = V[r], V[r + 1]
-        for a in tiles:
+        for a in where:
             rows, up, down = pl.ds(a, T8), pl.ds(a + 1, T8), pl.ds(a - 1, T8)
             own = pl.ds(a - PAD, T8)
-            halo = CP[rows, :]
+            halo = CP[rows, :] if ready else None
             m, mu, md = field[x0, rows, :], field[x0, up, :], field[x0, down, :]
             v, vu, vd = field[x0 + 1, rows, :], field[x0 + 1, up, :], field[x0 + 1, down, :]
             tv = zp(v)
@@ -437,7 +474,9 @@
                 q = (acc + f0 * n) + (F[1, p, rows, :] * vu + F[1, p, down, :] * vd)
                 q = q + (f3 * nu - f4d * nd) + (f2 * tv + f5 * tn)
                 q = q + (f7 * zp(vu) - f8d * zp(vd))
-                q = q + zm(s) + unpack(halo, x)
+                q = q + zm(s)
+                if ready:
+                    q = q + unpack(halo, x)
                 acc = (f0 * v + f3d * vd) - (f4 * vu + f6 * tv)
                 accs = f5 * v
                 odd = odd + v * q
@@ -447,10 +486,25 @@
                 v, vu, vd, tv = n, nu, nd, tn
         return odd, evn
 
-    def pairs(r, x0, width):
+    def settle(r, x0, width, where):
+        odd, evn = zero(), zero()
+        for a in where:
+            rows, own = pl.ds(a, T8), pl.ds(a - PAD, T8)
+            halo = CP[rows, :]
+            for i in range(width):
+                x = x0 + i
+                c = unpack(halo, x)
+                w = V[r + 1][x + 1, rows, :]
+                full = w + c * DI[x, own, :]
+                V[r + 1][x + 1, rows, :] = full
+                odd = odd + c * V[r][x + 1, rows, :]
+                evn = evn + c * (w + full)
+        return odd, evn
+
+    def pairs(r, x0, width, where):
         total = zero()
         field = V[r]
-        for a in tiles:
+        for a in where:
             rows, up = pl.ds(a, T8), pl.ds(a + 1, T8)
             v, vu = field[x0 + 1, rows, :], field[x0 + 1, up, :]
             tv, tvu = zp(v), zp(vu)
@@ -471,15 +525,14 @@
     def along_y(a):
         return pltpu.roll(a, YE - 1, 0) - pltpu.roll(a, 1, 0)
 
+    def sums(step, parts):
+        for i, part in enumerate(parts):
+            MA[2 * step + 1 + i] = MA[2 * step + 1 + i] + part
+
     sign = jnp.where(even, f32(-1.0), f32(1.0))
     for step in range(ITERS):
         r = step + 1
         last = step + 1 == ITERS
-        if step:
-            with scope(f"pack_{r}"):
-                pack(r, field_tile(r))
-            with scope(f"start_{r}"):
-                start_rest(r)
         if last:
             with scope("early_sums"):
                 tile = zero()
@@ -487,6 +540,28 @@
                     value = jnp.sum(jnp.sum(MA[k], axis=0, keepdims=True), axis=1, keepdims=True)
                     tile = jnp.where(lane_8 == k, value, tile)
                 CP[pl.ds(0, T8), :] = tile
+        with scope(f"inner_{r}"):
+            if last:
+                width = group_size(X - 2, 6)
+                MA[MOMENTS - 1] = pairs(r, X - 2, 1, tiles[:-1])
+
+                @pl.loop(0, (X - 2) // width)
+                def _(g):
+                    MA[MOMENTS - 1] = MA[MOMENTS - 1] + pairs(r, g * width, width, tiles[:-1])
+            else:
+                width = group_size(X - 2, 6)
+
+                @pl.loop(0, (X - 2) // width)
+                def _(g):
+                    sums(step, planes(r, 1 + g * width, width, tiles[1:-1], False))
+
+        if not last:
+            with scope(f"pack_in_{r}"):
+                for k in range(1, KT - 1):
+                    PS[r + 1, pl.ds(PAD + T8 * k, T8), :] = packed(field_tile(r + 1), k, 1, X - 1)
+                if not step:
+                    for k in range(1, KT - 1):
+                        DP[pl.ds(PAD + T8 * k, T8), :] = packed(lambda x, k: DI[x, pl.ds(T8 * k, T8), :], k, 1, X - 1)
         with scope(f"wait_{r}"):
             wait(r)
         with scope(f"halo_{r}"):
@@ -499,33 +574,44 @@
         if last:
             break
         with scope(f"edge_{r}"):
-            o0, e0 = planes(r, 0, 1)
-            o1, e1 = planes(r, X - 1, 1)
-            MA[2 * step + 1] = o0 + o1
-            MA[2 * step + 2] = e0 + e1
+            sums(step, planes(r, 0, 1, tiles))
+            sums(step, planes(r, X - 1, 1, tiles))
         with scope(f"startx_{r + 1}"):
             start_x(r + 1, field_tile(r + 1))
-        with scope(f"matvec_{r}"):
-            width = group_size(X - 2, 6)
+        with scope(f"rim_{r}"):
+            width = group_size(X - 2, 15)
 
             @pl.loop(0, (X - 2) // width)
             def _(g):
-                odd, evn = planes(r, 1 + g * width, width)
-                MA[2 * step + 1] = MA[2 * step + 1] + odd
-                MA[2 * step + 2] = MA[2 * step + 2] + evn
+                sums(step, planes(r, 1 + g * width, width, (PAD, TOP - T8)))
+
+        with scope(f"pack_{r + 1}"):
+            for k in range(KT):
+                rows = pl.ds(PAD + T8 * k, T8)
+                if k in (0, KT - 1):
+                    tile = packed(field_tile(r + 1), k, 0, X)
+                else:
+                    tile = PS[r + 1, rows, :] + CP[rows, :] * DP[rows, :]
+                    tile = jnp.where(lane_8 >= 2 * X - 3, pltpu.roll(V[r + 1][X, rows, :], 2 * X - 2, 1), tile)
+                    tile = jnp.where(ends, V[r + 1][1, rows, :], tile)
+                PS[r + 1, rows, :] = tile
+            spread(r + 1)
+        with scope(f"start_{r + 1}"):
+            start_rest(r + 1)
+        with scope(f"settle_{r}"):
+            width = group_size(X - 2, 6)
+
+            @pl.loop(0, (X - 2) // width)
+            def _(g):
+                sums(step, settle(r, 1 + g * width, width, tiles[1:-1]))
 
     with scope("pairs"):
-        width = group_size(X, 8)
         mine = jnp.logical_and(lane_8 % 2 == 1, jnp.logical_or(lane_8 < 2 * (X - 1), lane_8 == LANES - 1))
-        total = zero()
+        total = pairs(ROUNDS - 1, X - 1, 1, tiles)
         for a in tiles:
             rows = pl.ds(a, T8)
             total = total + jnp.where(mine, PS[ROUNDS - 1, rows, :] * CP[rows, :], 0.0)
-        MA[MOMENTS - 1] = total
-
-        @pl.loop(0, X // width)
-        def _(g):
-            MA[MOMENTS - 1] = MA[MOMENTS - 1] + pairs(ROUNDS - 1, g * width, width)
+        MA[MOMENTS - 1] = MA[MOMENTS - 1] + (total + pairs(ROUNDS - 1, 0, X - 1, (TOP - T8,)))
 
     def leave():
         wait_sent(ROUNDS - 1)
@@ -651,6 +737,7 @@
                 vmem((3, YE, Z), f32),
                 vmem((3, YE, Z), f32),
                 vmem((YE, Z), f32),
+                vmem((YE, Z), f32),
                 vmem((MOMENTS, 8, Z), f32),
                 vmem((2, 1, Z), f32),
                 vmem((2, 32, 1, Z), f32),
@@ -658,7 +745,7 @@
                 pltpu.SemaphoreType.DMA((2, 18)),
                 pltpu.SemaphoreType.DMA((orders,)),
                 pltpu.SemaphoreType.DMA((orders,)),
-                pltpu.SemaphoreType.DMA((3,)),
+                pltpu.SemaphoreType.DMA((5,)),
             ],
             compiler_params=pltpu.CompilerParams(
                 collective_id=0, has_side_effects=True, vmem_limit_bytes=60 * 1024 * 1024

time: 31.8 us -> 28.4 us (0.89)
  Pallas kernels: 31.7 us -> 28.2 us
    pallas_call x1, Pallas kernels: 30.6 us -> 27.2 us  [local(): pl.pallas_call(functools.partial(kernel, sizes), out_shape=(vmem((ITERS,...]
where the time goes in v3:
time: 28.4 us; the launch traced here: 28.2 us
  Pallas kernels  28.2 us (99%)
    pallas_call x1, Pallas kernels, local(): pl.pallas_call(functools.partial(kernel, sizes), out_shape=(vmem((ITERS,...  27.2 us
    pallas_call x1, Pallas kernels, local(): pl.pallas_call(combine, out_shape=jax.ShapeDtypeStruct((X, Y, Z), f32), i...  1.05 us

profile of v3, /device:TPU:0, one launch (start us, length us, event | category | flops | bytes accessed | tf_op | source)
XLA Modules:
  0.0 28.2 jit_solution(13698225772246082448)
XLA Ops:
  0.0 27.2 %shard_map.37 = (f32[3,32,64,128]{3,2,1,0:T(8,128)S(1)}, f32[8,128]{1,0:T(8,128)S(1)}) custom-call(s32[32,64,128]{2,1,0:T(8,128)} %lab_hbm.1, f32[7,8]{1,0:T(8,128)} %cond_hbm.1, f32[32,64,128]{2,1,0:T(8,128)} %rhs_hbm.1), custom_call_target="tpu_custom_call" | custom-call | tf_op jit(solution)/shard_map/pallas_call | solution.py:710
  27.2 1.0 %shard_map.38 = f32[32,64,128]{2,1,0:T(8,128)} custom-call(f32[3,32,64,128]{3,2,1,0:T(8,128)S(1)} %get-tuple-element.7.W, f32[8,128]{1,0:T(8,128)S(1)} %get-tuple-element.8.C), custom_call_target="tpu_custom_call" | custom-call | tf_op jit(solution)/shard_map/pallas_call | solution.py:754

commit v4 on v3

--- a/solution.py
+++ b/solution.py
@@ -57,6 +57,11 @@
                 if live in (1, 2) and all(n > 1 for t, n in zip(d, sizes) if t):
                     directions.append(d)
 
+    def opposite(d):
+        return tuple(-t for t in d)
+
+    axes_of = [d for d in directions if d > opposite(d)]
+
     def needed(d, r):
         if r < ROUNDS - 1:
             return True
@@ -92,7 +97,7 @@
 
     def copy(d, r):
         src, dst = places(d, r)
-        m = directions.index(d)
+        m = axes_of.index(max(d, opposite(d)))
         return pltpu.make_async_remote_copy(
             src_ref=src,
             dst_ref=dst,
@@ -172,8 +177,18 @@
     inner = lane_8 < LANES - 1
     tiles = [PAD + T8 * k for k in range(KT)]
 
+    by_row = lax.GatherDimensionNumbers(
+        offset_dims=(),
+        collapsed_slice_dims=(0,),
+        start_index_map=(0,),
+        operand_batching_dims=(1,),
+        start_indices_batching_dims=(1,),
+    )
+
     def look(c, index):
-        return jnp.take_along_axis(tables[c], index, axis=0, mode="promise_in_bounds")
+        return lax.gather(
+            tables[c], index[..., None], by_row, (1, 1), mode=lax.GatherScatterMode.PROMISE_IN_BOUNDS
+        )
 
     def look_known(values, components):
         index = jnp.maximum(values.astype(jnp.int32) - 1, 0)
@@ -205,18 +220,43 @@
             if not d[0]:
                 send(d, r)
 
+    def two(d):
+        dx, dy, dz = map(abs, d)
+        if dx + dy + dz == 2:
+            return F.at[0, 0, pl.ds(0, 2 * T8 if dx and dz else 2)]
+        if dz:
+            return F.at[0, 0, pl.ds(0, Y // 2)]
+        return F.at[0, pl.ds(0, 2), pl.ds(0, Y)] if dx else F.at[0, pl.ds(0, X), pl.ds(0, 2)]
+
+    def settle_pair(d, r, sent):
+        back = opposite(d)
+        ways = [t for t in (d, back) if needed(t, r)]
+        here = [present(t if sent else opposite(t)) for t in ways]
+
+        def one():
+            c = copy(ways[0], r)
+            c.wait_send() if sent else c.wait_recv()
+
+        if len(ways) == 1:
+            pl.when(here[0])(one)
+        elif ways:
+            sems = send_sem if sent else recv_sem
+
+            @pl.when(jnp.logical_and(*here))
+            def _():
+                pltpu.make_async_copy(two(d), two(d), sems.at[r % 2, axes_of.index(d)]).wait()
+
+            pl.when(jnp.logical_xor(*here))(one)
+
     def wait_sent(r):
-        for d in directions:
-            if needed(d, r):
-                pl.when(present(d))(lambda d=d: copy(d, r).wait_send())
+        for d in axes_of:
+            settle_pair(d, r, True)
 
     def wait(r):
         if r:
             wait_sent(r - 1)
-        for d in directions:
-            if needed(d, r):
-                back = tuple(-t for t in d)
-                pl.when(present(back))(lambda d=d: copy(d, r).wait_recv())
+        for d in axes_of:
+            settle_pair(d, r, False)
 
     def spread(r):
         for side in range(2):
@@ -320,13 +360,19 @@
         tables.append(table)
 
 
+    def sigma_own(x, where):
+        for a in where:
+            index = lab[x, pl.ds(a - PAD, T8), :]
+            for c in range(6):
+                S[c, x + 1, pl.ds(a, T8), :] = look(c, index)
+
     with scope("sigma_own"):
         @pl.loop(0, X, unroll=4)
         def _(x):
-            for a in tiles:
-                index = lab[x, pl.ds(a - PAD, T8), :]
-                for c in range(6):
-                    S[c, x + 1, pl.ds(a, T8), :] = look(c, index)
+            sigma_own(x, tiles[:2] + tiles[-2:])
+
+        for x in (0, 1, X - 2, X - 1):
+            sigma_own(x, tiles[2:-2])
 
     def coefficients(p, where, inside=True):
         for a in where:
@@ -349,14 +395,58 @@
                     s2 = S[2, p, rows, :]
                     F[2, p, rows, :] = jnp.where(inner, s2 + zp(s2), 0.0)
 
+    def inside_of(x0, width, where):
+        for a in where:
+            rows = pl.ds(a, T8)
+            own, up, down = (pl.ds(a - PAD + i, T8) for i in (0, 1, -1))
+            here, above = lab[x0, own, :], lab[x0, up, :]
+            s0, s3, s4, s3u = look(0, here), look(3, here), look(4, here), look(3, above)
+            f0m = look(0, lab[x0 - 1, own, :]) + s0
+            for i in range(width):
+                x = x0 + i
+                p = x + 1
+                there, beyond = lab[x + 1, own, :], lab[x + 1, up, :]
+                n0, n3, n4, n3u = look(0, there), look(3, there), look(4, there), look(3, beyond)
+                s1, s2, s5 = look(1, here), look(2, here), look(5, here)
+                s1u, s5u = look(1, above), look(5, above)
+                f0, f1 = s0 + n0, s1 + s1u
+                f2 = jnp.where(inner, s2 + zp(s2), 0.0)
+                F[0, p, rows, :] = f0
+                F[1, p, rows, :] = f1
+                F[2, p, rows, :] = f2
+                F[3, p, rows, :] = s3 + n3u
+                F[4, p, rows, :] = n3 + s3u
+                F[5, p, rows, :] = jnp.where(inner, s4 + zp(n4), 0.0)
+                F[6, p, rows, :] = jnp.where(inner, n4 + zp(s4), 0.0)
+                F[7, p, rows, :] = jnp.where(inner, s5 + zp(s5u), 0.0)
+                F[8, p, rows, :] = jnp.where(inner, s5u + zp(s5), 0.0)
+                diag = (look(6, here) + (f0m + f0)) + (f1 + (s1 + look(1, lab[x, down, :])))
+                DI[x, own, :] = diag + ((f2 + zm(f2)) + jnp.where(ends, s2, 0.0))
+                here, above, f0m = there, beyond, f0
+                s0, s3, s4, s3u = n0, n3, n4, n3u
+
     with scope("coef_in"):
-        width = group_size(X - 2, 3)
+        width = group_size(X - 2, 5)
+        for t in range(1, KT - 1, 3):
+            @pl.loop(0, (X - 2) // width)
+            def _(g, t=t):
+                inside_of(1 + g * width, width, tiles[t : min(t + 3, KT - 1)])
+
+        coefficients(1, tiles[1:-1])
+        width = group_size(X - 2, 10)
 
         @pl.loop(0, (X - 2) // width)
         def _(g):
             for i in range(width):
-                coefficients(1 + g * width + i, tiles[:-1])
-        coefficients(X - 1, tiles[:-1])
+                coefficients(1 + g * width + i, tiles[:1])
+        coefficients(X - 1, tiles[:1])
+
+    with scope("pack_d"):
+        rhs_copy.wait()
+        for k in range(1, KT - 1):
+            rows = pl.ds(PAD + T8 * k, T8)
+            DP[rows, :] = packed(lambda x, k: DI[x, pl.ds(T8 * k, T8), :], k, 1, X - 1)
+            PS[1, rows, :] = packed(lambda x, k: rhs[x, pl.ds(T8 * k, T8), :], k, 1, X - 1)
 
     with scope("wait0"):
         wait(0)
@@ -378,11 +468,10 @@
         for x in range(1, X + 1):
             for a in (0, TOP):
                 sigma_halo(x, pl.ds(a, T8), (1,))
-        rhs_copy.wait()
-
-    def diagonal(x, total):
+
+    def diagonal(x, total, where):
         p = x + 1
-        for a in tiles:
+        for a in where:
             rows, up, down = pl.ds(a, T8), pl.ds(a + 1, T8), pl.ds(a - 1, T8)
             own = pl.ds(a - PAD, T8)
             s2 = S[2, p, rows, :]
@@ -403,24 +492,57 @@
         return jnp.zeros((T8, LANES), f32)
 
     with scope("diag_x"):
-        MA[0] = diagonal(X - 1, diagonal(0, zero()))
+        MA[0] = diagonal(X - 1, diagonal(0, zero(), tiles), tiles)
     with scope("startx_1"):
         start_x(1, field_tile(1))
-    with scope("diag"):
-        width = group_size(X - 2, 6)
+    with scope("diag_rim"):
+        width = group_size(X - 2, 15)
 
         @pl.loop(0, (X - 2) // width)
         def _(g):
             total = zero()
             for i in range(width):
-                total = diagonal(1 + g * width + i, total)
+                total = diagonal(1 + g * width + i, total, (PAD, TOP - T8))
             MA[0] = MA[0] + total
 
+    def assemble(r, known):
+        for k in range(KT):
+            rows = pl.ds(PAD + T8 * k, T8)
+            if k in (0, KT - 1):
+                tile = packed(field_tile(r), k, 0, X)
+            else:
+                tile = jnp.where(lane_8 >= 2 * X - 3, pltpu.roll(V[r][X, rows, :], 2 * X - 2, 1), known(rows))
+                tile = jnp.where(ends, V[r][1, rows, :], tile)
+            PS[r, rows, :] = tile
+        spread(r)
+
+    def first(rows):
+        inverse = 1.0 / (DP[rows, :] + CP[rows, :])
+        DP[rows, :] = inverse
+        return PS[1, rows, :] * inverse
+
     with scope("pack_1"):
-        pack(1, field_tile(1))
-        spread(1)
+        assemble(1, first)
     with scope("start_1"):
         start_rest(1)
+    with scope("diag_in"):
+        width = group_size(X - 2, 10)
+
+        @pl.loop(0, (X - 2) // width)
+        def _(g):
+            total = zero()
+            for a in tiles[1:-1]:
+                own, halo = pl.ds(a - PAD, T8), CP[pl.ds(a, T8), :]
+                for i in range(width):
+                    x = 1 + g * width + i
+                    inverse = 1.0 / (DI[x, own, :] + unpack(halo, x))
+                    DI[x, own, :] = inverse
+                    r0 = rhs[x, own, :]
+                    w = r0 * inverse
+                    V[1][x + 1, pl.ds(a, T8), :] = w
+                    total = total + r0 * w
+            MA[0] = MA[0] + total
+
     with scope("coef"):
         for rows in halo_tiles:
             for i, s in enumerate(look_known(HB[rows, :], (4, 5))):
@@ -542,14 +664,14 @@
                 CP[pl.ds(0, T8), :] = tile
         with scope(f"inner_{r}"):
             if last:
-                width = group_size(X - 2, 6)
+                width = group_size(X - 2, 10)
                 MA[MOMENTS - 1] = pairs(r, X - 2, 1, tiles[:-1])
 
                 @pl.loop(0, (X - 2) // width)
                 def _(g):
                     MA[MOMENTS - 1] = MA[MOMENTS - 1] + pairs(r, g * width, width, tiles[:-1])
             else:
-                width = group_size(X - 2, 6)
+                width = group_size(X - 2, 10)
 
                 @pl.loop(0, (X - 2) // width)
                 def _(g):
@@ -559,9 +681,6 @@
             with scope(f"pack_in_{r}"):
                 for k in range(1, KT - 1):
                     PS[r + 1, pl.ds(PAD + T8 * k, T8), :] = packed(field_tile(r + 1), k, 1, X - 1)
-                if not step:
-                    for k in range(1, KT - 1):
-                        DP[pl.ds(PAD + T8 * k, T8), :] = packed(lambda x, k: DI[x, pl.ds(T8 * k, T8), :], k, 1, X - 1)
         with scope(f"wait_{r}"):
             wait(r)
         with scope(f"halo_{r}"):
@@ -586,20 +705,11 @@
                 sums(step, planes(r, 1 + g * width, width, (PAD, TOP - T8)))
 
         with scope(f"pack_{r + 1}"):
-            for k in range(KT):
-                rows = pl.ds(PAD + T8 * k, T8)
-                if k in (0, KT - 1):
-                    tile = packed(field_tile(r + 1), k, 0, X)
-                else:
-                    tile = PS[r + 1, rows, :] + CP[rows, :] * DP[rows, :]
-                    tile = jnp.where(lane_8 >= 2 * X - 3, pltpu.roll(V[r + 1][X, rows, :], 2 * X - 2, 1), tile)
-                    tile = jnp.where(ends, V[r + 1][1, rows, :], tile)
-                PS[r + 1, rows, :] = tile
-            spread(r + 1)
+            assemble(r + 1, lambda rows: PS[r + 1, rows, :] + CP[rows, :] * DP[rows, :])
         with scope(f"start_{r + 1}"):
             start_rest(r + 1)
         with scope(f"settle_{r}"):
-            width = group_size(X - 2, 6)
+            width = group_size(X - 2, 15)
 
             @pl.loop(0, (X - 2) // width)
             def _(g):
@@ -741,8 +851,8 @@
                 vmem((MOMENTS, 8, Z), f32),
                 vmem((2, 1, Z), f32),
                 vmem((2, 32, 1, Z), f32),
-                pltpu.SemaphoreType.DMA((2, 18)),
-                pltpu.SemaphoreType.DMA((2, 18)),
+                pltpu.SemaphoreType.DMA((2, 9)),
+                pltpu.SemaphoreType.DMA((2, 9)),
                 pltpu.SemaphoreType.DMA((orders,)),
                 pltpu.SemaphoreType.DMA((orders,)),
                 pltpu.SemaphoreType.DMA((5,)),

time: 28.4 us -> 27.6 us (0.972)
  Pallas kernels: 28.2 us -> 27.4 us
    pallas_call x1, Pallas kernels: 27.2 us -> 26.4 us  [local(): pl.pallas_call(functools.partial(kernel, sizes), out_shape=(vmem((ITERS,...]
where the time goes in v4:
time: 27.6 us; the launch traced here: 27.5 us
  Pallas kernels  27.4 us (99%)
    pallas_call x1, Pallas kernels, local(): pl.pallas_call(functools.partial(kernel, sizes), out_shape=(vmem((ITERS,...  26.4 us
    pallas_call x1, Pallas kernels, local(): pl.pallas_call(combine, out_shape=jax.ShapeDtypeStruct((X, Y, Z), f32), i...  1.05 us

profile of v4, /device:TPU:0, one launch (start us, length us, event | category | flops | bytes accessed | tf_op | source)
XLA Modules:
  0.0 27.5 jit_solution(14620106246081258752)
XLA Ops:
  0.0 26.4 %shard_map.37 = (f32[3,32,64,128]{3,2,1,0:T(8,128)S(1)}, f32[8,128]{1,0:T(8,128)S(1)}) custom-call(s32[32,64,128]{2,1,0:T(8,128)} %lab_hbm.1, f32[7,8]{1,0:T(8,128)} %cond_hbm.1, f32[32,64,128]{2,1,0:T(8,128)} %rhs_hbm.1), custom_call_target="tpu_custom_call" | custom-call | tf_op jit(solution)/shard_map/pallas_call | solution.py:820
  26.4 1.0 %shard_map.38 = f32[32,64,128]{2,1,0:T(8,128)} custom-call(f32[3,32,64,128]{3,2,1,0:T(8,128)S(1)} %get-tuple-element.7.W, f32[8,128]{1,0:T(8,128)S(1)} %get-tuple-element.8.C), custom_call_target="tpu_custom_call" | custom-call | tf_op jit(solution)/shard_map/pallas_call | solution.py:864

commit v5 on v4

--- a/solution.py
+++ b/solution.py
@@ -27,7 +27,7 @@
 
 def kernel(
     sizes, lab_hbm, cond_hbm, rhs_hbm, W, C, lab, cond, rhs, V0, V1, V2, V3, S, F, DI, PS, PZ, PR, ZR, ES, ER, HB, HS, PG, CP,
-    DP, MA, RS, RR, send_sem, recv_sem, ar_send, ar_recv, in_sem,
+    DP, K, MA, RS, RR, send_sem, recv_sem, ar_send, ar_recv, in_sem,
 ):
     V = (V0, V1, V2, V3)
     X, Y, Z = rhs.shape
@@ -169,10 +169,8 @@
         V[0][x, pl.ds(TOP + 1, PAD - 1), :] = jnp.zeros((PAD - 1, LANES), f32)
     MA[...] = jnp.zeros(MA.shape, f32)
 
-    lane_e = lax.broadcasted_iota(jnp.int32, (YE, LANES), 1)
     lane_8 = lax.broadcasted_iota(jnp.int32, (T8, LANES), 1)
     row_8 = lax.broadcasted_iota(jnp.int32, (T8, LANES), 0)
-    even = lane_e % 2 == 0
     ends = jnp.logical_or(lane_8 == 0, lane_8 == LANES - 1)
     inner = lane_8 < LANES - 1
     tiles = [PAD + T8 * k for k in range(KT)]
@@ -196,6 +194,7 @@
         return [jnp.where(hit, look(c, index), 0.0) for c in components]
 
     half = LANES // 2
+    span = LANES - 2 - 2 * X
     offs = (0, 1, half, half + 1)
     slots_of = [jnp.logical_and(lane_8 % 2 == off % 2, (lane_8 < half) == (off < half)) for off in offs]
 
@@ -205,15 +204,23 @@
 
     def start_x(r, plane):
         tile = jnp.zeros((T8, LANES), f32)
-        for col, (x, at) in enumerate(((0, 0), (0, LANES - 1), (X - 1, 0), (X - 1, LANES - 1))):
+        for x, base in ((0, 0), (X - 1, span)):
             for k in range(KT):
-                to = col * KT + k
-                part = plane(x, k)
-                tile = jnp.where(lane_8 == to, pltpu.roll(part, (to - at) % LANES, 1), tile)
+                to = base + 2 * k
+                here = jnp.logical_or(lane_8 == to, lane_8 == to + 1)
+                tile = jnp.where(here, pltpu.roll(plane(x, k), to + 1, 1), tile)
         ES[r] = tile
-        for d in sorted(directions, key=lambda d: (-abs(d[2]), -abs(d[1]))):
-            if d[0]:
-                send(d, r)
+        outer = sorted((d for d in directions if d[0]), key=lambda d: (-abs(d[2]), -abs(d[1])))
+
+        def both(side):
+            for t in (side, -side):
+                for d in outer:
+                    if d[0] == t:
+                        send(d, r)
+
+        far = lax.rem(me[0], 2) == 1
+        pl.when(far)(lambda: both(1))
+        pl.when(jnp.logical_not(far))(lambda: both(-1))
 
     def start_rest(r):
         for d in sorted(directions, key=lambda d: (-abs(d[2]), -abs(d[1]))):
@@ -286,18 +293,15 @@
             low = None if last else pltpu.roll(ZR[r, 0, t, :], (LANES - off) % LANES, 1)
             high = pltpu.roll(ZR[r, 1, t, :], LANES - 1 - off, 1)
             HB[pl.ds(PAD + T8 * k, T8), :] = join(low, high)
-        targets = (((LANES - 2), 3), ((LANES - 3), 2), (2 * X, 1), (2 * X - 1, 0))
-        slots = (1, 3) if last else (0, 1, 2, 3)
-        got = {slot: ER[r, slot] for slot in slots}
+        got = [(1, jnp.where(lane_8 < span, ER[r, 3], ER[r, 1]))]
+        if not last:
+            got.append((0, jnp.where(lane_8 < span, ER[r, 2], ER[r, 0])))
         for k in range(KT):
             rows = pl.ds(PAD + T8 * k, T8)
             part = HB[rows, :]
-            for slot in slots:
-                target, col = targets[slot]
-                at = col * KT + k
-                part = jnp.where(
-                    lane_8 == target, pltpu.roll(got[slot], (target - at) % LANES, 1), part
-                )
+            for i, tile in got:
+                here = jnp.logical_or(lane_8 == 2 * X - i, lane_8 == LANES - 2 - i)
+                part = jnp.where(here, pltpu.roll(tile, (2 * X - 2 * i - 2 * k) % LANES, 1), part)
             HB[rows, :] = part
 
     def zm(a):
@@ -433,14 +437,6 @@
                 inside_of(1 + g * width, width, tiles[t : min(t + 3, KT - 1)])
 
         coefficients(1, tiles[1:-1])
-        width = group_size(X - 2, 10)
-
-        @pl.loop(0, (X - 2) // width)
-        def _(g):
-            for i in range(width):
-                coefficients(1 + g * width + i, tiles[:1])
-        coefficients(X - 1, tiles[:1])
-
     with scope("pack_d"):
         rhs_copy.wait()
         for k in range(1, KT - 1):
@@ -496,14 +492,10 @@
     with scope("startx_1"):
         start_x(1, field_tile(1))
     with scope("diag_rim"):
-        width = group_size(X - 2, 15)
-
-        @pl.loop(0, (X - 2) // width)
-        def _(g):
-            total = zero()
-            for i in range(width):
-                total = diagonal(1 + g * width + i, total, (PAD, TOP - T8))
-            MA[0] = MA[0] + total
+        total = MA[0]
+        for x in range(1, X - 1):
+            total = diagonal(x, total, (PAD, TOP - T8))
+        MA[0] = total
 
     def assemble(r, known):
         for k in range(KT):
@@ -551,6 +543,15 @@
                 PG[i, rows, :] = s
             for x in (0, X + 1):
                 sigma_halo(x, rows, (3, 4))
+        sign = jnp.where(lane_8 % 2 == 0, f32(-1.0), f32(1.0))
+        for a in tiles:
+            rows = pl.ds(a, T8)
+            own, beside, above = PG[1, rows, :], HS[1, rows, :], PG[2, rows, :]
+            K[0, rows, :] = PG[0, rows, :] + HS[0, rows, :]
+            K[1, rows, :] = sign * (own + pltpu.roll(beside, LANES - 2, 1))
+            K[2, rows, :] = -sign * (own + pltpu.roll(beside, 2, 1))
+            K[3, rows, :] = sign * (above + HS[2, pl.ds(a + 1, T8), :])
+            K[4, rows, :] = -sign * (above + HS[2, pl.ds(a - 1, T8), :])
 
         @pl.loop(1, X + 1, unroll=4)
         def _(x):
@@ -559,13 +560,13 @@
 
         coefficients(0, [0] + tiles, False)
         coefficients(X, [0] + tiles)
-        coefficients(X - 1, (0, TOP - T8))
+        coefficients(X - 1, (0, PAD, TOP - T8))
         width = group_size(X - 2, 10)
 
         @pl.loop(0, (X - 2) // width)
         def _(g):
             for i in range(width):
-                coefficients(1 + g * width + i, (0, TOP - T8))
+                coefficients(1 + g * width + i, (0, PAD, TOP - T8))
 
     def planes(r, x0, width, where, ready=True):
         odd, evn = zero(), zero()
@@ -641,17 +642,10 @@
                 v, vu, tv, tvu = n, nu, tn, tnu
         return total
 
-    def along_x(a):
-        return pltpu.roll(a, LANES - 2, 1) - pltpu.roll(a, 2, 1)
-
-    def along_y(a):
-        return pltpu.roll(a, YE - 1, 0) - pltpu.roll(a, 1, 0)
-
     def sums(step, parts):
         for i, part in enumerate(parts):
             MA[2 * step + 1 + i] = MA[2 * step + 1 + i] + part
 
-    sign = jnp.where(even, f32(-1.0), f32(1.0))
     for step in range(ITERS):
         r = step + 1
         last = step + 1 == ITERS
@@ -685,11 +679,13 @@
             wait(r)
         with scope(f"halo_{r}"):
             build_halo(r)
-            h = HB[...]
-            full = (PG[0] + HS[0]) * h + sign * (
-                PG[1] * along_x(h) + along_x(HS[1] * h) + PG[2] * along_y(h) + along_y(HS[2] * h)
-            )
-            CP[pl.ds(PAD, Y), :] = full[PAD:TOP]
+            for a in tiles:
+                rows = pl.ds(a, T8)
+                h = HB[rows, :]
+                total = K[0, rows, :] * h + K[1, rows, :] * pltpu.roll(h, LANES - 2, 1)
+                total = total + K[2, rows, :] * pltpu.roll(h, 2, 1)
+                total = total + K[3, rows, :] * HB[pl.ds(a + 1, T8), :]
+                CP[rows, :] = total + K[4, rows, :] * HB[pl.ds(a - 1, T8), :]
         if last:
             break
         with scope(f"edge_{r}"):
@@ -698,11 +694,7 @@
         with scope(f"startx_{r + 1}"):
             start_x(r + 1, field_tile(r + 1))
         with scope(f"rim_{r}"):
-            width = group_size(X - 2, 15)
-
-            @pl.loop(0, (X - 2) // width)
-            def _(g):
-                sums(step, planes(r, 1 + g * width, width, (PAD, TOP - T8)))
+            sums(step, planes(r, 1, X - 2, (PAD, TOP - T8)))
 
         with scope(f"pack_{r + 1}"):
             assemble(r + 1, lambda rows: PS[r + 1, rows, :] + CP[rows, :] * DP[rows, :])
@@ -848,6 +840,7 @@
                 vmem((3, YE, Z), f32),
                 vmem((YE, Z), f32),
                 vmem((YE, Z), f32),
+                vmem((5, YE, Z), f32),
                 vmem((MOMENTS, 8, Z), f32),
                 vmem((2, 1, Z), f32),
                 vmem((2, 32, 1, Z), f32),

time: 27.6 us -> 26.8 us (0.971)
  Pallas kernels: 27.4 us -> 26.6 us
    pallas_call x1, Pallas kernels: 26.4 us -> 25.6 us  [local(): pl.pallas_call(functools.partial(kernel, sizes), out_shape=(vmem((ITERS,...]
where the time goes in v5:
time: 26.8 us; the launch traced here: 26.6 us
  Pallas kernels  26.6 us (99%)
    pallas_call x1, Pallas kernels, local(): pl.pallas_call(functools.partial(kernel, sizes), out_shape=(vmem((ITERS,...  25.6 us
    pallas_call x1, Pallas kernels, local(): pl.pallas_call(combine, out_shape=jax.ShapeDtypeStruct((X, Y, Z), f32), i...  1.05 us

profile of v5, /device:TPU:0, one launch (start us, length us, event | category | flops | bytes accessed | tf_op | source)
XLA Modules:
  0.0 26.6 jit_solution(2468230466621677328)
XLA Ops:
  0.0 25.6 %shard_map.37 = (f32[3,32,64,128]{3,2,1,0:T(8,128)S(1)}, f32[8,128]{1,0:T(8,128)S(1)}) custom-call(s32[32,64,128]{2,1,0:T(8,128)} %lab_hbm.1, f32[7,8]{1,0:T(8,128)} %cond_hbm.1, f32[32,64,128]{2,1,0:T(8,128)} %rhs_hbm.1), custom_call_target="tpu_custom_call" | custom-call | tf_op jit(solution)/shard_map/pallas_call | solution.py:812
  25.6 1.0 %shard_map.38 = f32[32,64,128]{2,1,0:T(8,128)} custom-call(f32[3,32,64,128]{3,2,1,0:T(8,128)S(1)} %get-tuple-element.7.W, f32[8,128]{1,0:T(8,128)S(1)} %get-tuple-element.8.C), custom_call_target="tpu_custom_call" | custom-call | tf_op jit(solution)/shard_map/pallas_call | solution.py:857

commit v6 on v5

--- a/solution.py
+++ b/solution.py
@@ -364,19 +364,21 @@
         tables.append(table)
 
 
-    def sigma_own(x, where):
+    def sigma_own(x, where, components=range(6)):
         for a in where:
             index = lab[x, pl.ds(a - PAD, T8), :]
-            for c in range(6):
+            for c in components:
                 S[c, x + 1, pl.ds(a, T8), :] = look(c, index)
 
     with scope("sigma_own"):
         @pl.loop(0, X, unroll=4)
         def _(x):
-            sigma_own(x, tiles[:2] + tiles[-2:])
+            sigma_own(x, (tiles[0], tiles[-1]))
+            sigma_own(x, (tiles[1],), (1, 3, 5))
+            sigma_own(x, (tiles[-2],), (1,))
 
         for x in (0, 1, X - 2, X - 1):
-            sigma_own(x, tiles[2:-2])
+            sigma_own(x, tiles[1:-1])
 
     def coefficients(p, where, inside=True):
         for a in where:

time: 26.8 us -> 26.8 us (level)
  no operation moved by 1% of the time
where the time goes in v6:
time: 26.8 us; the launch traced here: 26.6 us
  Pallas kernels  26.6 us (99%)
    pallas_call x1, Pallas kernels, local(): pl.pallas_call(functools.partial(kernel, sizes), out_shape=(vmem((ITERS,...  25.6 us
    pallas_call x1, Pallas kernels, local(): pl.pallas_call(combine, out_shape=jax.ShapeDtypeStruct((X, Y, Z), f32), i...  1.05 us

profile of v6, /device:TPU:0, one launch (start us, length us, event | category | flops | bytes accessed | tf_op | source)
XLA Modules:
  0.0 26.6 jit_solution(1562644264505165855)
XLA Ops:
  0.0 25.6 %shard_map.37 = (f32[3,32,64,128]{3,2,1,0:T(8,128)S(1)}, f32[8,128]{1,0:T(8,128)S(1)}) custom-call(s32[32,64,128]{2,1,0:T(8,128)} %lab_hbm.1, f32[7,8]{1,0:T(8,128)} %cond_hbm.1, f32[32,64,128]{2,1,0:T(8,128)} %rhs_hbm.1), custom_call_target="tpu_custom_call" | custom-call | tf_op jit(solution)/shard_map/pallas_call | solution.py:814
  25.6 1.0 %shard_map.38 = f32[32,64,128]{2,1,0:T(8,128)} custom-call(f32[3,32,64,128]{3,2,1,0:T(8,128)S(1)} %get-tuple-element.7.W, f32[8,128]{1,0:T(8,128)S(1)} %get-tuple-element.8.C), custom_call_target="tpu_custom_call" | custom-call | tf_op jit(solution)/shard_map/pallas_call | solution.py:859
